TPU v7x, 32 devices: a whole 2x2x4 slice. The times are simulated.
32 devices in a mesh: lat: 4 (over x, core), lon: 2 (over y), lev: 4 (over z).
Axes of the slice: x: 2, y: 2, z: 4, core: 2. Of those that a mesh axis runs over, the one named last changes fastest.
Arguments:
- outer_increment: bfloat16 [16, 256, 1024], P('lev', 'lat', 'lon'), may hold values from -6 to 6
- courant: bfloat16 [3, 16, 64, 256], P(None, 'lev', 'lat', 'lon'), may hold values from -0.29882812 to 0.29882812
- obs_column: int32 [16384], P(('lat', 'lon')), may hold values from 0 to 2047
- obs_level: int32 [16384], P(('lat', 'lon')), may hold values from 0 to 15
- obs_value: float32 [16384], P(('lat', 'lon')), may hold values from -6 to 6
Outputs:
- inner_state: float32 [16, 64, 256], P('lev', 'lat', 'lon')
- adjoint: float32 [16, 64, 256], P('lev', 'lat', 'lon')
- outer_next: bfloat16 [16, 256, 1024], P('lev', 'lat', 'lon')
Inputs may be any that keep to these rules, and one draw needn't show every extreme that they name: obs_column numbers a column of the 16 x 512 / 4 inner block of its latitude-longitude block, row by row.
All inputs are finite; a program needn't handle non-finite values.
Results may differ from a plain program's by a relative error of at most 0.001.
Values sent between devices are 32-bit elements; how exact they have to be, the bound alone decides.
A program may use at most 64 MiB of HBM per device.

v0:
```python
import functools

import jax
import jax.numpy as jnp
from jax import lax
from jax.experimental import pallas as pl
from jax.experimental.pallas import tpu as pltpu
from jax.sharding import PartitionSpec as P

MESH = pl.DeviceIdType.MESH
ROUNDS = 3


def bf16_parts(x, count):
    parts = []
    for _ in range(count):
        part = x.astype(jnp.bfloat16).astype(jnp.float32)
        parts.append(part)
        x = x - part
    return parts


def kernel(
    ends, outer_hbm, courant_hbm, col_hbm, lvl_hbm, val_hbm,
    state_v, adj_v, outer,
    courant, col, lvl, val, sums,
    lev_out, lat_out, lon_out, lev_in, lat_in, lon_in,
    lev2_out, lat2_out, edge_out, pack_out, lev2_in, lat2_in, edge_in, pack_in,
    in_sem, send_sem, recv_sem, send2_sem, recv2_sem,
):
    n_lat, n_lon, n_lev = ends
    levels, rows, cols = state_v.shape
    flat_rows = levels * rows
    wide_cols = outer.shape[1]
    fine = wide_cols // cols

    loads = [
        pltpu.make_async_copy(src, dst, in_sem.at[i])
        for i, (src, dst) in enumerate(
            ((outer_hbm, outer), (courant_hbm, courant), (col_hbm, col), (lvl_hbm, lvl), (val_hbm, val))
        )
    ]
    for load in loads:
        load.start()

    me_lat, me_lon, me_lev = (lax.axis_index(a) for a in ("lat", "lon", "lev"))
    links = (
        ("lev", me_lev + 1, me_lev < n_lev - 1),
        ("lev", me_lev - 1, me_lev > 0),
        ("lat", me_lat + 1, me_lat < n_lat - 1),
        ("lat", me_lat - 1, me_lat > 0),
        ("lon", lax.rem(me_lon + 1, n_lon), None),
        ("lon", lax.rem(me_lon + n_lon - 1, n_lon), None),
    )
    side_lev = (links[0], links[1])
    side_lat = (links[2], links[3])
    side_lon = (links[4], links[5])

    def joined(*sides):
        exists = [e for _, _, e in sides if e is not None]
        target = {axis: who for axis, who, _ in sides}
        return target, functools.reduce(jnp.logical_and, exists) if exists else None

    wide_links = []

    def add(sides, opposite, source, landing):
        target, exists = joined(*sides)
        wide_links.append((target, exists, joined(*opposite)[1], source, landing))

    for s in range(2):
        add([side_lev[s]], [side_lev[1 - s]], lambda q, s=s: lev2_out.at[q, s], lambda q, s=s: lev2_in.at[q, s])
        add([side_lat[s]], [side_lat[1 - s]], lambda q, s=s: lat2_out.at[q, s], lambda q, s=s: lat2_in.at[q, s])
    for s in range(2):
        for t in range(2):
            add([side_lev[s], side_lat[t]], [side_lev[1 - s], side_lat[1 - t]],
                lambda q, e=2 * s + t: edge_out.at[q, e], lambda q, e=2 * s + t: edge_in.at[q, e])
    faces_end = len(wide_links)
    for u in range(2):
        add([side_lon[u]], [side_lon[1 - u]], lambda q: pack_out.at[q], lambda q, e=u: pack_in.at[q, e])
    for base, sides in ((2, side_lev), (6, side_lat)):
        for s in range(2):
            for u in range(2):
                add([sides[s], side_lon[u]], [sides[1 - s], side_lon[1 - u]],
                    lambda q: pack_out.at[q], lambda q, e=base + 2 * s + u: pack_in.at[q, e])
    outs = {"lev": lev_out, "lat": lat_out, "lon": lon_out}
    ins = {"lev": lev_in, "lat": lat_in, "lon": lon_in}

    def guarded(exists, action):
        if exists is None:
            action()
        else:
            pl.when(exists)(action)

    barrier = pltpu.get_barrier_semaphore()
    for target, exists, _, _, _ in wide_links:
        guarded(
            exists,
            lambda target=target: pl.semaphore_signal(
                barrier, inc=1, device_id=target, device_id_type=MESH
            ),
        )

    def wide_message(q, i):
        target, _, _, source, landing = wide_links[i]
        return pltpu.make_async_remote_copy(
            src_ref=source(q),
            dst_ref=landing(q),
            send_sem=send2_sem.at[q, i],
            recv_sem=recv2_sem.at[q, i],
            device_id=target,
            device_id_type=MESH,
        )

    def clear(landing):
        for q in range(2):
            ref = landing(q)
            ref[...] = jnp.zeros(ref.shape, jnp.float32)

    for _, _, arrives, _, landing in wide_links:
        if arrives is not None:
            pl.when(jnp.logical_not(arrives))(lambda landing=landing: clear(landing))

    def message(turn, which):
        axis, who, _ = links[which]
        side = which % 2
        source = outs[axis].at[turn] if axis == "lon" else outs[axis].at[turn, side]
        return pltpu.make_async_remote_copy(
            src_ref=source,
            dst_ref=ins[axis].at[turn, side],
            send_sem=send_sem.at[turn, which],
            recv_sem=recv_sem.at[turn, which],
            device_id={axis: who},
            device_id_type=MESH,
        )

    def blank(ref, side):
        for turn in range(ROUNDS):
            ref[turn, side] = jnp.zeros(ref.shape[2:], jnp.float32)

    pl.when(me_lev == 0)(lambda: blank(lev_in, 0))
    pl.when(me_lev == n_lev - 1)(lambda: blank(lev_in, 1))
    pl.when(me_lat == 0)(lambda: blank(lat_in, 0))
    pl.when(me_lat == n_lat - 1)(lambda: blank(lat_in, 1))

    lane = lax.broadcasted_iota(jnp.int32, (flat_rows, cols), 1)
    flat = lax.broadcasted_iota(jnp.int32, (flat_rows, cols), 0)
    lane3 = lax.broadcasted_iota(jnp.int32, (levels, rows, cols), 2)
    row3 = lax.broadcasted_iota(jnp.int32, (levels, rows, cols), 1)

    pool = (
        lax.broadcasted_iota(jnp.int32, (wide_cols, cols), 0) // fine
        == lax.broadcasted_iota(jnp.int32, (wide_cols, cols), 1)
    ).astype(jnp.float32).astype(jnp.bfloat16)

    def pack(first, last):
        first = first.reshape(flat_rows, cols)[:, :1]
        last = last.reshape(flat_rows, cols)[:, cols - 1 :]
        spread = jnp.where(lane == flat, first, 0.0) + jnp.where(lane == flat + flat_rows, last, 0.0)
        return jnp.sum(spread, axis=0, keepdims=True)

    def column(row, begin, step, length):
        at = lax.broadcasted_iota(jnp.int32, (length, cols), 1)
        index = lax.broadcasted_iota(jnp.int32, (length, cols), 0)
        return jnp.sum(jnp.where(at == begin + step * index, row, 0.0), axis=1, keepdims=True)

    def either(from_previous, from_next):
        at = lax.broadcasted_iota(jnp.int32, from_next.shape, 1)
        return jnp.where(at < flat_rows, from_next, from_previous)

    def ends_of(row):
        return [column(row, b, 1, flat_rows).reshape(levels, rows, 1) for b in (flat_rows, 0)]

    def shifted(firsts, lasts, lev, lat, lon):
        below = [
            jnp.concatenate([lev[0][None], lasts[0][: levels - 1]], axis=0),
            jnp.where(row3 == 0, lat[0][:, None, :], pltpu.roll(lasts[1], 1, axis=1)),
            jnp.where(lane3 == 0, lon[0], pltpu.roll(lasts[2], 1, axis=2)),
        ]
        above = [
            jnp.concatenate([firsts[0][1:], lev[1][None]], axis=0),
            jnp.where(row3 == rows - 1, lat[1][:, None, :], pltpu.roll(firsts[1], rows - 1, axis=1)),
            jnp.where(lane3 == cols - 1, lon[1], pltpu.roll(firsts[2], cols - 1, axis=2)),
        ]
        return below, above

    def send(turn, firsts, lasts):
        lev_out[turn, 0] = lasts[0][levels - 1]
        lev_out[turn, 1] = firsts[0][0]
        lat_out[turn, 0] = lasts[1][:, rows - 1, :]
        lat_out[turn, 1] = firsts[1][:, 0, :]
        for which in range(4):
            guarded(links[which][2], lambda which=which: message(turn, which).start())
        lon_out[turn] = pack(firsts[2], lasts[2])
        for which in (4, 5):
            message(turn, which).start()

    def receive(turn):
        for which in range(6):
            guarded(links[which ^ 1][2], lambda which=which: message(turn, which).wait_recv())
        return (
            [lev_in[turn, 0], lev_in[turn, 1]],
            [lat_in[turn, 0], lat_in[turn, 1]],
            either(lon_in[turn, 0], lon_in[turn, 1]),
        )

    expected = sum(1 if link[1] is None else link[1].astype(jnp.int32) for link in wide_links)
    loads[1].wait()
    numbers = courant[...].astype(jnp.float32)
    lower = [jnp.maximum(numbers[k], 0.0) for k in range(3)]
    upper = [jnp.maximum(-numbers[k], 0.0) for k in range(3)]
    centre = 1.0 - jnp.abs(numbers[0]) - jnp.abs(numbers[1]) - jnp.abs(numbers[2])

    loads[0].wait()
    sums[...] = jnp.dot(outer[...], pool, preferred_element_type=jnp.float32)
    coarse = sums[pl.ds(0, flat_rows, stride=fine), :]
    for k in range(1, fine):
        coarse = coarse + sums[pl.ds(k, flat_rows, stride=fine), :]
    coarse = (coarse * (1.0 / (fine * fine))).reshape(levels, rows, cols)

    lev3 = lax.broadcasted_iota(jnp.int32, (levels, rows, cols), 0)
    last_lev, last_row = levels - 1, rows - 1
    lev_edge = (last_lev, 0)
    row_edge = (last_row, 0)
    none_lev = jnp.zeros((rows, cols), jnp.float32)
    none_lat = jnp.zeros((levels, cols), jnp.float32)

    def step(values, lev, lat, lon):
        below, above = shifted([values] * 3, [values] * 3, lev, lat, lon)
        result = centre * values
        for k in range(3):
            result = result + lower[k] * below[k] + upper[k] * above[k]
        return result

    partial = step(coarse, [none_lev] * 2, [none_lat] * 2, [0.0, 0.0])
    pl.semaphore_wait(barrier, expected)
    for s in range(2):
        lev2_out[0, s, 0] = partial[lev_edge[s]]
        lev2_out[0, s, 1] = coarse[lev_edge[s]]
        lat2_out[0, s, 0] = partial[:, row_edge[s], :]
        lat2_out[0, s, 1] = coarse[:, row_edge[s], :]
        for t in range(2):
            for i in range(2):
                edge_out[0, 2 * s + t, i : i + 1] = coarse[lev_edge[s], row_edge[t] : row_edge[t] + 1, :]
    for i in range(faces_end):
        guarded(wide_links[i][1], lambda i=i: wide_message(0, i).start())
    own_pack = pack(coarse, coarse)
    pack_out[0, 0:1] = pack(partial, partial)
    pack_out[0, 1:2] = own_pack
    pack_out[0, 2:3] = own_pack
    pack_out[0, 3:4] = own_pack
    for i in range(faces_end, len(wide_links)):
        guarded(wide_links[i][1], lambda i=i: wide_message(0, i).start())

    for k in range(3):
        send(k, [numbers[k]] * 3, [numbers[k]] * 3)

    for load in loads[2:]:
        load.wait()
    where_row = (lvl[...] - me_lev * levels) * rows + col[...] // cols
    where_col = col[...] % cols
    parts = bf16_parts(val[...], 3)
    pieces, width = col.shape
    row_id = lax.broadcasted_iota(jnp.int32, (flat_rows, width), 0)
    col_id = lax.broadcasted_iota(jnp.int32, (cols, width), 0)
    hits = [[] for _ in range(4)]
    tables = []
    for k in range(pieces):
        match = where_row[k : k + 1] == row_id
        hits[0].append(jnp.where(match, 1.0, 0.0).astype(jnp.bfloat16))
        for i, part in enumerate(parts):
            hits[i + 1].append(jnp.where(match, part[k : k + 1], 0.0).astype(jnp.bfloat16))
        tables.append(jnp.where(where_col[k : k + 1] == col_id, 1.0, 0.0).astype(jnp.bfloat16))
    left_side = jnp.concatenate([jnp.concatenate(h, axis=1) for h in hits], axis=0)
    totals = lax.dot_general(
        left_side, jnp.concatenate(tables, axis=1), (((1,), (1,)), ((), ())),
        preferred_element_type=jnp.float32,
    )
    count = totals[:flat_rows].reshape(levels, rows, cols)
    observed = (
        totals[flat_rows : 2 * flat_rows]
        + totals[2 * flat_rows : 3 * flat_rows]
        + totals[3 * flat_rows :]
    ).reshape(levels, rows, cols)

    plane_row = lax.broadcasted_iota(jnp.int32, (rows, cols), 0)
    plane_lane = lax.broadcasted_iota(jnp.int32, (rows, cols), 1)
    line_lev = lax.broadcasted_iota(jnp.int32, (levels, cols), 0)
    line_lane = lax.broadcasted_iota(jnp.int32, (levels, cols), 1)
    at_lane = lax.broadcasted_iota(jnp.int32, (1, cols), 1)
    at = lax.rem(at_lane, flat_rows)
    at_lev, at_row = lax.div(at, rows), lax.rem(at, rows)

    def packs(q):
        return (
            either(pack_in[q, 0], pack_in[q, 1]),
            [either(pack_in[q, 2 + 2 * s], pack_in[q, 3 + 2 * s]) for s in range(2)],
            [either(pack_in[q, 6 + 2 * s], pack_in[q, 7 + 2 * s]) for s in range(2)],
        )

    speeds = [receive(k) for k in range(3)]

    def low(x):
        return jnp.maximum(x, 0.0)

    def up(x):
        return jnp.maximum(-x, 0.0)

    for i in range(len(wide_links)):
        guarded(wide_links[i][2], lambda i=i: wide_message(0, i).wait_recv())
    side_pack, lev_pack, lat_pack = packs(0)
    beside_lev, beside_lat = [], []
    for s in range(2):
        near, far = (up, low) if s == 0 else (low, up)
        c = [speeds[k][0][s] for k in range(3)]
        plane = lev2_in[0, s, 0] + near(c[0]) * coarse[(0, last_lev)[s]]
        plane = plane + jnp.where(plane_row == 0, low(c[1]) * edge_in[0, 2 * s, 0:1], 0.0)
        plane = plane + jnp.where(plane_row == last_row, up(c[1]) * edge_in[0, 2 * s + 1, 0:1], 0.0)
        begin = lev_edge[s] * rows
        moved = lev_pack[s][1:2]
        plane = plane + jnp.where(plane_lane == 0, low(c[2]) * column(moved, flat_rows + begin, 1, rows), 0.0)
        plane = plane + jnp.where(plane_lane == cols - 1, up(c[2]) * column(moved, begin, 1, rows), 0.0)
        beside_lev.append(plane)

        c = [speeds[k][1][s] for k in range(3)]
        plane = lat2_in[0, s, 0] + near(c[1]) * coarse[:, (0, last_row)[s], :]
        plane = plane + jnp.where(line_lev == 0, low(c[0]) * edge_in[0, s, 1:2], 0.0)
        plane = plane + jnp.where(line_lev == last_lev, up(c[0]) * edge_in[0, 2 + s, 1:2], 0.0)
        begin = row_edge[s]
        moved = lat_pack[s][1:2]
        plane = plane + jnp.where(
            line_lane == 0, low(c[2]) * column(moved, flat_rows + begin, rows, levels), 0.0
        )
        plane = plane + jnp.where(line_lane == cols - 1, up(c[2]) * column(moved, begin, rows, levels), 0.0)
        beside_lat.append(plane)
    c = [speeds[k][2] for k in range(3)]
    ring = side_pack[0:1] + jnp.where(at_lane < flat_rows, low(c[2]), up(c[2])) * pltpu.roll(
        own_pack, flat_rows, axis=1
    )
    turned = [pltpu.roll(lev_pack[0][1:2], cols - last_lev * rows, axis=1), pltpu.roll(lev_pack[1][1:2], last_lev * rows, axis=1)]
    ring = ring + jnp.where(at_lev == 0, low(c[0]) * turned[0], 0.0)
    ring = ring + jnp.where(at_lev == last_lev, up(c[0]) * turned[1], 0.0)
    turned = [pltpu.roll(lat_pack[0][1:2], cols - last_row, axis=1), pltpu.roll(lat_pack[1][1:2], last_row, axis=1)]
    ring = ring + jnp.where(at_row == 0, low(c[1]) * turned[0], 0.0)
    ring = ring + jnp.where(at_row == last_row, up(c[1]) * turned[1], 0.0)

    state = step(
        coarse, [lev2_in[0, s, 1] for s in range(2)], [lat2_in[0, s, 1] for s in range(2)],
        ends_of(side_pack[1:2]),
    )
    state = step(state, beside_lev, beside_lat, ends_of(ring))
    field = count * state - observed

    state_v[...] = state
    to_first = [lower[k] * field for k in range(3)]
    to_last = [upper[k] * field for k in range(3)]
    below, above = shifted(to_first, to_last, [none_lev] * 2, [none_lat] * 2, [0.0, 0.0])
    partial = centre * field
    for k in range(3):
        partial = partial + above[k] + below[k]

    last_lev, last_row = levels - 1, rows - 1
    lev_edge = (last_lev, 0)
    row_edge = (last_row, 0)
    for s in range(2):
        lev_move = (to_last, to_first)[s]
        lev2_out[1, s, 0] = partial[lev_edge[s]]
        lev2_out[1, s, 1] = lev_move[0][lev_edge[s]]
        lat2_out[1, s, 0] = partial[:, row_edge[s], :]
        lat2_out[1, s, 1] = lev_move[1][:, row_edge[s], :]
        for t in range(2):
            lat_move = (to_last, to_first)[t]
            r = row_edge[t]
            edge_out[1, 2 * s + t, 0:1] = lat_move[1][lev_edge[s], r : r + 1, :]
            edge_out[1, 2 * s + t, 1:2] = lev_move[0][lev_edge[s], r : r + 1, :]
    for i in range(faces_end):
        guarded(wide_links[i][1], lambda i=i: wide_message(1, i).start())
    moved_lon = pack(to_first[2], to_last[2])
    at_lev_ends = jnp.where(lev3 == 0, to_first[0], jnp.where(lev3 == last_lev, to_last[0], 0.0))
    at_row_ends = jnp.where(row3 == 0, to_first[1], jnp.where(row3 == last_row, to_last[1], 0.0))
    pack_out[1, 0:1] = pack(partial, partial)
    pack_out[1, 1:2] = moved_lon
    pack_out[1, 2:3] = pack(at_lev_ends, at_lev_ends)
    pack_out[1, 3:4] = pack(at_row_ends, at_row_ends)
    for i in range(faces_end, len(wide_links)):
        guarded(wide_links[i][1], lambda i=i: wide_message(1, i).start())

    speed_lev = [up(speeds[0][0][0]), low(speeds[0][0][1])]
    speed_lat = [up(speeds[1][1][0]), low(speeds[1][1][1])]
    speed_lon = jnp.where(at_lane < flat_rows, low(speeds[2][2]), up(speeds[2][2]))
    for i in range(len(wide_links)):
        guarded(wide_links[i][2], lambda i=i: wide_message(1, i).wait_recv())
    side_pack, lev_pack, lat_pack = packs(1)

    left, right = ends_of(side_pack[1:2])
    field = partial + jnp.where(lane3 == 0, left, 0.0) + jnp.where(lane3 == cols - 1, right, 0.0)
    field = field + jnp.where(lev3 == 0, lev2_in[1, 0, 1][None], 0.0)
    field = field + jnp.where(lev3 == last_lev, lev2_in[1, 1, 1][None], 0.0)
    field = field + jnp.where(row3 == 0, lat2_in[1, 0, 1][:, None, :], 0.0)
    field = field + jnp.where(row3 == last_row, lat2_in[1, 1, 1][:, None, :], 0.0)

    plane_row = lax.broadcasted_iota(jnp.int32, (rows, cols), 0)
    plane_lane = lax.broadcasted_iota(jnp.int32, (rows, cols), 1)
    line_lev = lax.broadcasted_iota(jnp.int32, (levels, cols), 0)
    line_lane = lax.broadcasted_iota(jnp.int32, (levels, cols), 1)
    beside_lev, beside_lat = [], []
    for s in range(2):
        own = (to_first[0][0], to_last[0][last_lev])[s]
        plane = lev2_in[1, s, 0] + own
        plane = plane + jnp.where(plane_row == 0, edge_in[1, 2 * s, 0:1], 0.0)
        plane = plane + jnp.where(plane_row == last_row, edge_in[1, 2 * s + 1, 0:1], 0.0)
        begin = lev_edge[s] * rows
        moved = lev_pack[s][1:2]
        plane = plane + jnp.where(plane_lane == 0, column(moved, flat_rows + begin, 1, rows), 0.0)
        plane = plane + jnp.where(plane_lane == cols - 1, column(moved, begin, 1, rows), 0.0)
        beside_lev.append(plane * speed_lev[s])

        own = (to_first[1][:, 0, :], to_last[1][:, last_row, :])[s]
        plane = lat2_in[1, s, 0] + own
        plane = plane + jnp.where(line_lev == 0, edge_in[1, s, 1:2], 0.0)
        plane = plane + jnp.where(line_lev == last_lev, edge_in[1, 2 + s, 1:2], 0.0)
        begin = row_edge[s]
        moved = lat_pack[s][1:2]
        plane = plane + jnp.where(line_lane == 0, column(moved, flat_rows + begin, rows, levels), 0.0)
        plane = plane + jnp.where(line_lane == cols - 1, column(moved, begin, rows, levels), 0.0)
        beside_lat.append(plane * speed_lat[s])
    at = lax.rem(lax.broadcasted_iota(jnp.int32, (1, cols), 1), flat_rows)
    at_lev, at_row = lax.div(at, rows), lax.rem(at, rows)
    ring = side_pack[0:1] + pltpu.roll(moved_lon, flat_rows, axis=1)
    ring = ring + jnp.where(at_lev == 0, pltpu.roll(lev_pack[0][2:3], cols - last_lev * rows, axis=1), 0.0)
    ring = ring + jnp.where(at_lev == last_lev, pltpu.roll(lev_pack[1][2:3], last_lev * rows, axis=1), 0.0)
    ring = ring + jnp.where(at_row == 0, pltpu.roll(lat_pack[0][3:4], cols - last_row, axis=1), 0.0)
    ring = ring + jnp.where(at_row == last_row, pltpu.roll(lat_pack[1][3:4], last_row, axis=1), 0.0)
    beside_lon = ends_of(ring * speed_lon)

    below, above = shifted(
        [lower[k] * field for k in range(3)], [upper[k] * field for k in range(3)],
        beside_lev, beside_lat, beside_lon,
    )
    result = centre * field
    for k in range(3):
        result = result + above[k] + below[k]
    field = result
    adj_v[...] = field

    for turn in range(ROUNDS):
        for which in range(6):
            guarded(links[which][2], lambda turn=turn, which=which: message(turn, which).wait_send())
    for q in range(2):
        for i in range(len(wide_links)):
            guarded(wide_links[i][1], lambda q=q, i=i: wide_message(q, i).wait_send())


def finish(state_v, adj_v, outer, state_hbm, adj_hbm, next_hbm, wide, nxt, out_sem):
    levels, rows, cols = state_v.shape
    flat_rows = levels * rows
    wide_cols = outer.shape[1]
    fine = wide_cols // cols
    outer_rows = outer.shape[0] // levels
    stores = [
        pltpu.make_async_copy(state_v, state_hbm, out_sem.at[0]),
        pltpu.make_async_copy(adj_v, adj_hbm, out_sem.at[1]),
    ]
    for store in stores:
        store.start()
    field = adj_v[...]

    table = (
        lax.broadcasted_iota(jnp.int32, (cols, wide_cols), 0)
        == lax.broadcasted_iota(jnp.int32, (cols, wide_cols), 1) // fine
    ).astype(jnp.float32).astype(jnp.bfloat16)
    halves = bf16_parts(field.reshape(flat_rows, cols), 2)
    spread = jnp.dot(
        jnp.concatenate([h.astype(jnp.bfloat16) for h in halves], axis=1),
        jnp.concatenate([table, table], axis=0),
        preferred_element_type=jnp.float32,
    )
    for k in range(fine):
        for c in range(fine):
            wide[c, pl.ds(k, flat_rows, stride=fine), :] = spread[:, c * cols : (c + 1) * cols]
    for level in range(levels):
        span = pl.ds(level * outer_rows, outer_rows)
        for c in range(fine):
            lanes = pl.ds(c * cols, cols)
            nxt[span, lanes] = (outer[span, lanes].astype(jnp.float32) - wide[c, span, :]).astype(jnp.bfloat16)
        store = pltpu.make_async_copy(nxt.at[span], next_hbm.at[span], out_sem.at[2 + level])
        store.start()
        stores.append(store)
    for store in stores:
        store.wait()


def shards(ends, outer_increment, courant, obs_column, obs_level, obs_value):
    levels, outer_rows, wide_cols = outer_increment.shape
    _, _, rows, cols = courant.shape
    flat_rows = levels * rows
    fine = wide_cols // cols
    lanes = 128
    observed = (obs_column.shape[0] // lanes, lanes)
    assert 2 * flat_rows == cols and levels > 1 and rows > 1
    f32, bf16 = jnp.float32, jnp.bfloat16
    outer_shape = (levels * outer_rows, wide_cols)
    vmem = pl.BlockSpec(memory_space=pltpu.VMEM)
    hbm = pl.BlockSpec(memory_space=pl.ANY)
    held = pl.pallas_call(
        functools.partial(kernel, ends),
        out_shape=(
            pltpu.VMEM((levels, rows, cols), f32),
            pltpu.VMEM((levels, rows, cols), f32),
            pltpu.VMEM(outer_shape, bf16),
        ),
        in_specs=[hbm] * 5,
        out_specs=(vmem,) * 3,
        scratch_shapes=[
            pltpu.VMEM(courant.shape, bf16),
            pltpu.VMEM(observed, jnp.int32),
            pltpu.VMEM(observed, jnp.int32),
            pltpu.VMEM(observed, f32),
            pltpu.VMEM((levels * outer_rows, cols), f32),
            pltpu.VMEM((ROUNDS, 2, rows, cols), f32),
            pltpu.VMEM((ROUNDS, 2, levels, cols), f32),
            pltpu.VMEM((ROUNDS, 1, cols), f32),
            pltpu.VMEM((ROUNDS, 2, rows, cols), f32),
            pltpu.VMEM((ROUNDS, 2, levels, cols), f32),
            pltpu.VMEM((ROUNDS, 2, 1, cols), f32),
            pltpu.VMEM((2, 2, 2, rows, cols), f32),
            pltpu.VMEM((2, 2, 2, levels, cols), f32),
            pltpu.VMEM((2, 4, 2, cols), f32),
            pltpu.VMEM((2, 4, cols), f32),
            pltpu.VMEM((2, 2, 2, rows, cols), f32),
            pltpu.VMEM((2, 2, 2, levels, cols), f32),
            pltpu.VMEM((2, 4, 2, cols), f32),
            pltpu.VMEM((2, 10, 4, cols), f32),
            pltpu.SemaphoreType.DMA((5,)),
            pltpu.SemaphoreType.DMA((ROUNDS, 6)),
            pltpu.SemaphoreType.DMA((ROUNDS, 6)),
            pltpu.SemaphoreType.DMA((2, 18)),
            pltpu.SemaphoreType.DMA((2, 18)),
        ],
        compiler_params=pltpu.CompilerParams(collective_id=0, has_side_effects=True),
    )(
        outer_increment.reshape(outer_shape),
        courant,
        obs_column.reshape(observed),
        obs_level.reshape(observed),
        obs_value.reshape(observed),
    )
    state, adjoint, following = pl.pallas_call(
        finish,
        out_shape=(
            jax.ShapeDtypeStruct((levels, rows, cols), f32),
            jax.ShapeDtypeStruct((levels, rows, cols), f32),
            jax.ShapeDtypeStruct(outer_shape, bf16),
        ),
        in_specs=[vmem] * 3,
        out_specs=(hbm,) * 3,
        scratch_shapes=[
            pltpu.VMEM((fine, levels * outer_rows, cols), f32),
            pltpu.VMEM(outer_shape, bf16),
            pltpu.SemaphoreType.DMA((2 + levels,)),
        ],
    )(*[pltpu.with_memory_space_constraint(x, pltpu.VMEM) for x in held])
    return state, adjoint, following.reshape(outer_increment.shape)


def solution(mesh):
    ends = tuple(mesh.shape[a] for a in ("lat", "lon", "lev"))
    block = P("lev", "lat", "lon")
    observed = P(("lat", "lon"))
    return jax.shard_map(
        functools.partial(shards, ends),
        mesh=mesh,
        in_specs=(block, P(None, "lev", "lat", "lon"), observed, observed, observed),
        out_specs=(block, block, block),
        check_vma=False,
    )
```

profile of v0, /device:TPU:0, one launch (start us, length us, event | category | flops | bytes accessed | tf_op | source)
XLA Modules:
  0.0 14.9 jit_solution(17077463713012069301)
XLA Ops:
  0.6 13.3 %shard_map.76 = (f32[4,16,128]{2,1,0:T(8,128)S(1)}, f32[4,16,128]{2,1,0:T(8,128)S(1)}, bf16[256,512]{1,0:T(8,128)(2,1)S(1)}) custom-call(bf16[256,512]{1,0:T(8,128)(2,1)} %bitcast.5, bf16[3,4,16,128]{3,2,1,0:T(8,128)(2,1)} %courant_hbm.1, s32[16,128]{1,0:T(8,128)} %bitcast.6, s32[16,128]{1,0:T(8,128)} %bitcast.7, f32[16,128]{1,0:T(8,128)} %bitcast.8), custom_call_target="tpu_custom_call" | custom-call | tf_op jit(solution)/shard_map/pallas_call | solution.py:504
  14.0 0.9 %shard_map.77 = (f32[4,16,128]{2,1,0:T(8,128)}, f32[4,16,128]{2,1,0:T(8,128)}, bf16[256,512]{1,0:T(8,128)(2,1)}) custom-call(f32[4,16,128]{2,1,0:T(8,128)S(1)} %get-tuple-element.9.state_v, f32[4,16,128]{2,1,0:T(8,128)S(1)} %get-tuple-element.10.adj_v, bf16[256,512]{1,0:T(8,128)(2,1)S(1)} %get-tuple-element.11.outer), custom_call_target="tpu_custom_call" | custom-call | tf_op jit(solution)/shard_map/pallas_call | solution.py:547
where the time goes:
time: 15.1 us; the launch traced here: 14.9 us
  Pallas kernels  14.3 us (95%)
  between operations  0.64 us (4%)
    pallas_call x1, Pallas kernels, shards(): pl.pallas_call(functools.partial(kernel, ends), out_shape=(pltpu.VMEM((le...  13.3 us
    pallas_call x1, Pallas kernels, shards(): pl.pallas_call(finish, out_shape=(jax.ShapeDtypeStruct((levels, rows, col...  0.94 us

commit v1 on v0

--- a/solution.py
+++ b/solution.py
@@ -26,7 +26,7 @@
     courant, col, lvl, val, sums,
     lev_out, lat_out, lon_out, lev_in, lat_in, lon_in,
     lev2_out, lat2_out, edge_out, pack_out, lev2_in, lat2_in, edge_in, pack_in,
-    in_sem, send_sem, recv_sem, send2_sem, recv2_sem,
+    units, in_sem, send_sem, recv_sem,
 ):
     n_lat, n_lon, n_lev = ends
     levels, rows, cols = state_v.shape
@@ -65,7 +65,8 @@
 
     def add(sides, opposite, source, landing):
         target, exists = joined(*sides)
-        wide_links.append((target, exists, joined(*opposite)[1], source, landing))
+        needs = tuple(w for w in range(4) if any(links[w] is side for side in sides))
+        wide_links.append((target, exists, joined(*opposite)[1], source, landing, needs))
 
     for s in range(2):
         add([side_lev[s]], [side_lev[1 - s]], lambda q, s=s: lev2_out.at[q, s], lambda q, s=s: lev2_in.at[q, s])
@@ -92,7 +93,7 @@
             pl.when(exists)(action)
 
     barrier = pltpu.get_barrier_semaphore()
-    for target, exists, _, _, _ in wide_links:
+    for target, exists, _, _, _, _ in wide_links:
         guarded(
             exists,
             lambda target=target: pl.semaphore_signal(
@@ -101,12 +102,12 @@
         )
 
     def wide_message(q, i):
-        target, _, _, source, landing = wide_links[i]
+        target, _, _, source, landing, _ = wide_links[i]
         return pltpu.make_async_remote_copy(
             src_ref=source(q),
             dst_ref=landing(q),
-            send_sem=send2_sem.at[q, i],
-            recv_sem=recv2_sem.at[q, i],
+            send_sem=send_sem,
+            recv_sem=recv_sem.at[q],
             device_id=target,
             device_id_type=MESH,
         )
@@ -116,7 +117,7 @@
             ref = landing(q)
             ref[...] = jnp.zeros(ref.shape, jnp.float32)
 
-    for _, _, arrives, _, landing in wide_links:
+    for _, _, arrives, _, landing, _ in wide_links:
         if arrives is not None:
             pl.when(jnp.logical_not(arrives))(lambda landing=landing: clear(landing))
 
@@ -127,8 +128,8 @@
         return pltpu.make_async_remote_copy(
             src_ref=source,
             dst_ref=ins[axis].at[turn, side],
-            send_sem=send_sem.at[turn, which],
-            recv_sem=recv_sem.at[turn, which],
+            send_sem=send_sem,
+            recv_sem=recv_sem.at[0],
             device_id={axis: who},
             device_id_type=MESH,
         )
@@ -194,9 +195,7 @@
         for which in (4, 5):
             message(turn, which).start()
 
-    def receive(turn):
-        for which in range(6):
-            guarded(links[which ^ 1][2], lambda which=which: message(turn, which).wait_recv())
+    def received(turn):
         return (
             [lev_in[turn, 0], lev_in[turn, 1]],
             [lat_in[turn, 0], lat_in[turn, 1]],
@@ -297,7 +296,6 @@
             [either(pack_in[q, 6 + 2 * s], pack_in[q, 7 + 2 * s]) for s in range(2)],
         )
 
-    speeds = [receive(k) for k in range(3)]
 
     def low(x):
         return jnp.maximum(x, 0.0)
@@ -305,8 +303,33 @@
     def up(x):
         return jnp.maximum(-x, 0.0)
 
-    for i in range(len(wide_links)):
-        guarded(wide_links[i][2], lambda i=i: wide_message(0, i).wait_recv())
+    def lines(ref):
+        total = 1
+        for n in ref.shape:
+            total = total * n
+        return total // cols
+
+    def settle(groups, sem, known=()):
+        if len(known) < 4:
+            for has in (True, False):
+                flag = links[len(known)][2]
+                pl.when(flag if has else jnp.logical_not(flag))(
+                    lambda has=has: settle(groups, sem, known + (has,))
+                )
+            return
+        total = sum(amount for needs, amount in groups if all(known[w] for w in needs))
+        view = units.at[pl.ds(0, total)]
+        pltpu.make_async_copy(view, view, sem).wait()
+
+    def narrow_lines(flip):
+        sizes = {"lev": rows, "lat": levels, "lon": 1}
+        return [((w ^ flip,) if w < 4 else (), ROUNDS * sizes[links[w][0]]) for w in range(6)]
+
+    def wide_lines(q, flip):
+        return [(tuple(w ^ flip for w in link[5]), lines(link[4](q))) for link in wide_links]
+
+    settle(narrow_lines(1) + wide_lines(0, 1), recv_sem.at[0])
+    speeds = [received(k) for k in range(3)]
     side_pack, lev_pack, lat_pack = packs(0)
     beside_lev, beside_lat = [], []
     for s in range(2):
@@ -387,8 +410,7 @@
     speed_lev = [up(speeds[0][0][0]), low(speeds[0][0][1])]
     speed_lat = [up(speeds[1][1][0]), low(speeds[1][1][1])]
     speed_lon = jnp.where(at_lane < flat_rows, low(speeds[2][2]), up(speeds[2][2]))
-    for i in range(len(wide_links)):
-        guarded(wide_links[i][2], lambda i=i: wide_message(1, i).wait_recv())
+    settle(wide_lines(1, 1), recv_sem.at[1])
     side_pack, lev_pack, lat_pack = packs(1)
 
     left, right = ends_of(side_pack[1:2])
@@ -442,12 +464,7 @@
     field = result
     adj_v[...] = field
 
-    for turn in range(ROUNDS):
-        for which in range(6):
-            guarded(links[which][2], lambda turn=turn, which=which: message(turn, which).wait_send())
-    for q in range(2):
-        for i in range(len(wide_links)):
-            guarded(wide_links[i][1], lambda q=q, i=i: wide_message(q, i).wait_send())
+    settle(narrow_lines(0) + wide_lines(0, 0) + wide_lines(1, 0), send_sem)
 
 
 def finish(state_v, adj_v, outer, state_hbm, adj_hbm, next_hbm, wide, nxt, out_sem):
@@ -530,11 +547,10 @@
             pltpu.VMEM((2, 2, 2, levels, cols), f32),
             pltpu.VMEM((2, 4, 2, cols), f32),
             pltpu.VMEM((2, 10, 4, cols), f32),
+            pltpu.VMEM((1024, 1, cols), f32),
             pltpu.SemaphoreType.DMA((5,)),
-            pltpu.SemaphoreType.DMA((ROUNDS, 6)),
-            pltpu.SemaphoreType.DMA((ROUNDS, 6)),
-            pltpu.SemaphoreType.DMA((2, 18)),
-            pltpu.SemaphoreType.DMA((2, 18)),
+            pltpu.SemaphoreType.DMA,
+            pltpu.SemaphoreType.DMA((2,)),
         ],
         compiler_params=pltpu.CompilerParams(collective_id=0, has_side_effects=True),
     )(

time: 15.1 us -> 14.1 us (0.934)
  Pallas kernels: 14.3 us -> 13.3 us
    pallas_call x1, Pallas kernels: 13.3 us -> 12.4 us  [shards(): pl.pallas_call(functools.partial(kernel, ends), out_shape=(pltpu.VMEM((le...]
where the time goes in v1:
time: 14.1 us; the launch traced here: 13.9 us
  Pallas kernels  13.3 us (94%)
  between operations  0.64 us (5%)
    pallas_call x1, Pallas kernels, shards(): pl.pallas_call(functools.partial(kernel, ends), out_shape=(pltpu.VMEM((le...  12.4 us
    pallas_call x1, Pallas kernels, shards(): pl.pallas_call(finish, out_shape=(jax.ShapeDtypeStruct((levels, rows, col...  0.94 us

profile of v1, /device:TPU:0, one launch (start us, length us, event | category | flops | bytes accessed | tf_op | source)
XLA Modules:
  0.0 13.9 jit_solution(10528004964206025627)
XLA Ops:
  0.6 12.4 %shard_map.76 = (f32[4,16,128]{2,1,0:T(8,128)S(1)}, f32[4,16,128]{2,1,0:T(8,128)S(1)}, bf16[256,512]{1,0:T(8,128)(2,1)S(1)}) custom-call(bf16[256,512]{1,0:T(8,128)(2,1)} %bitcast.5, bf16[3,4,16,128]{3,2,1,0:T(8,128)(2,1)} %courant_hbm.1, s32[16,128]{1,0:T(8,128)} %bitcast.6, s32[16,128]{1,0:T(8,128)} %bitcast.7, f32[16,128]{1,0:T(8,128)} %bitcast.8), custom_call_target="tpu_custom_call" | custom-call | tf_op jit(solution)/shard_map/pallas_call | solution.py:521
  13.0 0.9 %shard_map.77 = (f32[4,16,128]{2,1,0:T(8,128)}, f32[4,16,128]{2,1,0:T(8,128)}, bf16[256,512]{1,0:T(8,128)(2,1)}) custom-call(f32[4,16,128]{2,1,0:T(8,128)S(1)} %get-tuple-element.9.state_v, f32[4,16,128]{2,1,0:T(8,128)S(1)} %get-tuple-element.10.adj_v, bf16[256,512]{1,0:T(8,128)(2,1)S(1)} %get-tuple-element.11.outer), custom_call_target="tpu_custom_call" | custom-call | tf_op jit(solution)/shard_map/pallas_call | solution.py:563

commit v2 on v0

v2 whole, which is shorter than its diff:
```python
import functools

import jax
import jax.numpy as jnp
from jax import lax
from jax.experimental import pallas as pl
from jax.experimental.pallas import tpu as pltpu
from jax.sharding import PartitionSpec as P

MESH = pl.DeviceIdType.MESH
REACH = 4
GROUP = 2 * REACH
TILE = 8


def bf16_parts(x, count):
    parts = []
    for _ in range(count):
        part = x.astype(jnp.bfloat16).astype(jnp.float32)
        parts.append(part)
        x = x - part
    return parts


def forward(v, c, minus, plus):
    sizes = [jnp.abs(n) for n in c]
    result = (1.0 - sizes[0] - sizes[1] - sizes[2]) * v
    for k in range(3):
        result = result + sizes[k] * jnp.where(c[k] > 0.0, minus[k], plus[k])
    return result


def shares(p, c):
    low, up = [], []
    for n in c:
        moved = jnp.abs(n) * p
        low.append(jnp.where(n > 0.0, moved, 0.0))
        up.append(jnp.where(n > 0.0, 0.0, moved))
    return low, up


def centre_of(c):
    return 1.0 - jnp.abs(c[0]) - jnp.abs(c[1]) - jnp.abs(c[2])


def kernel(
    ends, outer_hbm, courant_hbm, col_hbm, lvl_hbm, val_hbm,
    state_v, adj_v, outer,
    courant, col, lvl, val, sums,
    own, face_in, last_in, side_in, edge_out, edge_in, halo,
    strip, strip_full, strip_half,
    seen, seen_in, seen_strip, seen_full, seen_half, units,
    in_sem, send_sem, recv_sem,
):
    n_lat, n_lon, n_lev = ends
    levels, rows, cols = state_v.shape
    flat_rows = levels * rows
    wide_cols = outer.shape[1]
    fine = wide_cols // cols
    near = REACH - 1
    span = seen.shape[0]
    beyond = (span - levels) // 2

    me_lat, me_lon, me_lev = (lax.axis_index(a) for a in ("lat", "lon", "lev"))
    links = (
        ("lev", me_lev + 1, me_lev < n_lev - 1),
        ("lev", me_lev - 1, me_lev > 0),
        ("lat", me_lat + 1, me_lat < n_lat - 1),
        ("lat", me_lat - 1, me_lat > 0),
        ("lon", lax.rem(me_lon + 1, n_lon), None),
        ("lon", lax.rem(me_lon + n_lon - 1, n_lon), None),
    )
    turns = (0, 1) if n_lon > 2 else (0,)
    bands = ((rows - TILE, TILE), (0, TILE))

    def both(flags):
        return functools.reduce(jnp.logical_and, flags) if flags else None

    def guarded(exists, action):
        if exists is None:
            action()
        else:
            pl.when(exists)(action)

    class Message:
        def __init__(self, which, source, landing, sem):
            self.needs = tuple(w for w in which if w < 4)
            self.target = {links[w][0]: links[w][1] for w in which}
            self.exists = both([links[w][2] for w in self.needs])
            self.arrives = both([links[w ^ 1][2] for w in self.needs])
            self.source, self.landing, self.sem = source, landing, sem

        def start(self):
            def begin():
                pltpu.make_async_remote_copy(
                    src_ref=self.source, dst_ref=self.landing, send_sem=send_sem, recv_sem=recv_sem.at[self.sem],
                    device_id=self.target, device_id_type=MESH,
                ).start()

            guarded(self.exists, begin)

        def lines(self):
            total = 1
            for n in self.landing.shape:
                total = total * n
            return total // cols

    partners, first, second = [], [], []
    for a in (2, 1, 0):
        for t in (0, 1, None):
            for u in turns + (None,):
                which = [a - 1] if a else []
                which = which + ([2 + t] if t is not None else []) + ([4 + u] if u is not None else [])
                if not which:
                    continue
                partners.append(which)
                b = 0 if u is None else u + 1
                if t is None:
                    first.append(Message(which, strip, strip_full.at[a, b], 0))
                else:
                    first.append(Message(which, strip.at[pl.ds(*bands[t])], strip_half.at[a, t, b], 0))
                if u is None:
                    if a and t is None:
                        begin = levels - near if a == 1 else 0
                        furthest = levels - REACH if a == 1 else near
                        first.append(Message(which, own.at[pl.ds(begin, near)], face_in.at[a - 1], 0))
                        first.append(Message(which, own.at[furthest, 0], last_in.at[a - 1], 0))
                    elif a:
                        first.append(Message(which, edge_out.at[a - 1, t], edge_in.at[a - 1, t], 0))
                    else:
                        first.append(Message(which, own.at[:, :, pl.ds(*bands[t])], side_in.at[t], 0))
                if not a:
                    if t is None:
                        second.append(Message(which, seen_strip, seen_full.at[u], 1))
                    else:
                        second.append(Message(which, seen_strip.at[:, pl.ds(*bands[t])], seen_half.at[t, b], 1))
                    if u is None:
                        kept = pl.ds(1, span - 2)
                        second.append(Message(which, seen.at[kept, :, pl.ds(*bands[t])], seen_in.at[t], 1))
    first.sort(key=lambda m: m.lines() - 64 * len(m.target))

    barrier = pltpu.get_barrier_semaphore()
    expected = 0
    for which in partners:
        exists = both([links[w][2] for w in which if w < 4])
        target = {links[w][0]: links[w][1] for w in which}
        guarded(exists, lambda target=target: pl.semaphore_signal(barrier, inc=1, device_id=target, device_id_type=MESH))
        expected = expected + (1 if exists is None else exists.astype(jnp.int32))

    loads = [
        pltpu.make_async_copy(src, dst, in_sem.at[i])
        for i, (src, dst) in enumerate(
            ((outer_hbm, outer), (courant_hbm, courant), (col_hbm, col), (lvl_hbm, lvl), (val_hbm, val))
        )
    ]
    for load in loads:
        load.start()

    def settle(messages, flip, sem, known=()):
        if len(known) < 4:
            for has in (True, False):
                flag = links[len(known)][2]
                pl.when(flag if has else jnp.logical_not(flag))(
                    lambda has=has: settle(messages, flip, sem, known + (has,))
                )
            return
        total = sum(m.lines() for m in messages if all(known[w ^ flip] for w in m.needs))
        view = units.at[pl.ds(0, total)]
        pltpu.make_async_copy(view, view, sem).wait()

    def clear(ref):
        ref[...] = jnp.zeros(ref.shape, jnp.float32)

    for m in first + second:
        if m.arrives is not None:
            pl.when(jnp.logical_not(m.arrives))(lambda m=m: clear(m.landing))
    clear(halo)

    lane = lax.broadcasted_iota(jnp.int32, (rows, cols), 1)
    group = lane // GROUP
    pool = (
        lax.broadcasted_iota(jnp.int32, (wide_cols, cols), 0) // fine
        == lax.broadcasted_iota(jnp.int32, (wide_cols, cols), 1)
    ).astype(jnp.float32).astype(jnp.bfloat16)

    loads[1].wait()
    for k in range(3):
        own[:, k + 1] = courant[k].astype(jnp.float32)
    loads[0].wait()
    sums[...] = jnp.dot(outer[...], pool, preferred_element_type=jnp.float32)
    coarse = sums[pl.ds(0, flat_rows, stride=fine), :]
    for k in range(1, fine):
        coarse = coarse + sums[pl.ds(k, flat_rows, stride=fine), :]
    own[:, 0] = (coarse * (1.0 / (fine * fine))).reshape(levels, rows, cols)

    ends_only = jnp.zeros((rows, cols), jnp.float32)
    for f in (1, 2, 3, 0):
        for l in range(levels):
            place = f * levels + l
            ends_only = jnp.where(group == place, pltpu.roll(own[l, f], (REACH + GROUP * place) % cols, axis=1), ends_only)
    strip[...] = ends_only

    entries = [(0, i, j) for i in range(1, REACH) for j in range(1, REACH + 1 - i)]
    entries = entries + [(f, i, j) for f in (1, 2, 3) for i in range(1, near) for j in range(1, near + 1 - i)]
    for s in range(2):
        for t in range(2):
            for n, (f, i, j) in enumerate(entries):
                l = levels - i if s == 0 else i - 1
                r = rows - j if t == 0 else j - 1
                edge_out[s, t, n : n + 1, :] = own[l, f, r : r + 1, :]

    pl.semaphore_wait(barrier, expected)
    for m in first:
        m.start()

    for load in loads[2:]:
        load.wait()
    where_row = (lvl[...] - me_lev * levels + beyond) * rows + col[...] // cols
    where_col = col[...] % cols
    parts = bf16_parts(val[...], 2)
    pieces, width = col.shape
    row_id = lax.broadcasted_iota(jnp.int32, (span * rows, width), 0)
    col_id = lax.broadcasted_iota(jnp.int32, (cols, width), 0)
    hits = [[] for _ in range(3)]
    tables = []
    for k in range(pieces):
        match = where_row[k : k + 1] == row_id
        hits[0].append(jnp.where(match, 1.0, 0.0).astype(jnp.bfloat16))
        for i, part in enumerate(parts):
            hits[i + 1].append(jnp.where(match, part[k : k + 1], 0.0).astype(jnp.bfloat16))
        tables.append(jnp.where(where_col[k : k + 1] == col_id, 1.0, 0.0).astype(jnp.bfloat16))
    left_side = jnp.concatenate([jnp.concatenate(h, axis=1) for h in hits], axis=0)
    totals = lax.dot_general(
        left_side, jnp.concatenate(tables, axis=1), (((1,), (1,)), ((), ())),
        preferred_element_type=jnp.float32,
    )
    wide_rows = span * rows
    counted = totals[:wide_rows].reshape(span, rows, cols)
    summed = (totals[wide_rows : 2 * wide_rows] + totals[2 * wide_rows :]).reshape(span, rows, cols)
    seen[:, 0] = counted
    seen[:, 1] = summed
    for i, values in enumerate((counted, summed)):
        ends_only = jnp.zeros((rows, cols), jnp.float32)
        for g in range(span):
            place = g + REACH - beyond
            ends_only = jnp.where(group == place, pltpu.roll(values[g], (REACH + GROUP * place) % cols, axis=1), ends_only)
        seen_strip[i] = ends_only
    for m in second:
        m.start()

    settle(first, 1, recv_sem.at[0])

    tall = rows + TILE
    half = lax.broadcasted_iota(jnp.int32, (TILE, cols), 0) < TILE // 2
    lanes = lax.broadcasted_iota(jnp.int32, (tall, cols), 1)
    slot = lanes % GROUP
    left_half = slot < REACH
    blank = jnp.zeros((TILE, cols), jnp.float32)

    def joined(full, before, after):
        return jnp.concatenate([full, jnp.where(half, after, before)], axis=0)

    for s in range(2):
        for t in range(2):
            for n, (f, i, j) in enumerate(entries):
                r = TILE - j if t == 0 else j - 1
                halo[s, i - 1, f, r : r + 1, :] = edge_in[s, t, n : n + 1, :]

    def cell(l, f):
        if 0 <= l < levels:
            return joined(own[l, f], side_in[0, l, f], side_in[1, l, f])
        s, i = (0, -l) if l < 0 else (1, l - levels + 1)
        if i == REACH:
            return jnp.concatenate([last_in[s], blank], axis=0)
        full = face_in[s, near - i, f] if s == 0 else face_in[s, i - 1, f]
        return jnp.concatenate([full, halo[s, i - 1, f]], axis=0)

    def down(x):
        return pltpu.roll(x, 1, axis=0)

    def up_row(x):
        return pltpu.roll(x, tall - 1, axis=0)

    def right(x, by=1):
        return pltpu.roll(x, by, axis=1)

    def left(x, by=1):
        return pltpu.roll(x, cols - by, axis=1)

    before_b, after_b = 1, (2 if n_lon > 2 else 1)

    def strip_block(a, b):
        full = strip[...] if a == 0 and b == 0 else strip_full[a, b]
        return joined(full, strip_half[a, 0, b], strip_half[a, 1, b])

    def placed(blocks, f):
        turned = [right(blocks[a], (GROUP * levels * (n - f)) % cols) if n != f else blocks[a] for n, a in enumerate((1, 0, 2))]
        width = GROUP * levels
        return jnp.where(lanes < width, turned[0], jnp.where(lanes < 2 * width, turned[1], turned[2]))

    mine = [strip_block(a, 0) for a in range(3)]
    sides = []
    sides.append([jnp.where(left_half, strip_block(a, before_b), mine[a]) for a in range(3)])
    sides.append([jnp.where(left_half, mine[a], strip_block(a, after_b)) for a in range(3)])
    side_c, side_v = [], []
    for blocks in sides:
        c = [placed(blocks, k + 1) for k in range(3)]
        v = placed(blocks, 0)
        for _ in range(2):
            v = forward(v, c, [right(v, GROUP), down(v), right(v)], [left(v, GROUP), up_row(v), left(v)])
        side_c.append(c)
        side_v.append(v)

    def inserted(z, l):
        return right(z, (cols - REACH - GROUP * (l + REACH)) % cols)

    speeds = {l: [cell(l, k + 1) for k in range(3)] for l in range(-near, levels + near)}
    v = {l: cell(l, 0) for l in range(-REACH, levels + REACH)}
    for reach in (near, near - 1):
        v = {
            l: forward(v[l], speeds[l], [v[l - 1], down(v[l]), right(v[l])], [v[l + 1], up_row(v[l]), left(v[l])])
            for l in range(-reach, levels + reach)
        }
    fix = jnp.where(left_half, side_v[1], side_v[0])
    rim = (lanes < 2) | (lanes >= cols - 2)
    v = {l: jnp.where(rim, inserted(fix, l), v[l]) for l in v}
    for l in range(levels):
        state_v[l] = v[l][:rows]

    settle(second, 1, recv_sem.at[1])

    def seen_cell(l, i):
        g = l + beyond
        if 0 < g < span - 1:
            return joined(seen[g, i], seen_in[0, g - 1, i], seen_in[1, g - 1, i])
        return jnp.concatenate([seen[g, i], blank], axis=0)

    def seen_block(b, i):
        full = seen_strip[i] if b == 0 else seen_full[b - 1, i]
        return joined(full, seen_half[0, b, i], seen_half[1, b, i])

    side_q = []
    for side in range(2):
        known = []
        for i in range(2):
            if side == 0:
                known.append(jnp.where(left_half, seen_block(before_b, i), seen_block(0, i)))
            else:
                known.append(jnp.where(left_half, seen_block(0, i), seen_block(after_b, i)))
        p = known[0] * side_v[side] - known[1]
        c = side_c[side]
        low, up = shares(p, c)
        q = centre_of(c) * p + left(low[0], GROUP) + right(up[0], GROUP)
        q = q + up_row(low[1]) + down(up[1]) + left(low[2]) + right(up[2])
        low, up = shares(q, c)
        side_q.append((q, right(up[2]) if side == 0 else left(low[2])))
    fix = jnp.where(left_half, side_q[1][0], side_q[0][0])
    crossing = jnp.where(left_half, side_q[1][1], side_q[0][1])

    p = {l: seen_cell(l, 0) * v[l] - seen_cell(l, 1) for l in v}
    low, up = {}, {}
    for l in p:
        low[l], up[l] = shares(p[l], speeds[l])
    rim = (lanes < 1) | (lanes >= cols - 1)
    q = {}
    for l in range(-1, levels + 1):
        total = centre_of(speeds[l]) * p[l] + low[l + 1][0] + up[l - 1][0]
        total = total + up_row(low[l][1]) + down(up[l][1]) + left(low[l][2]) + right(up[l][2])
        q[l] = jnp.where(rim, inserted(fix, l), total)
    for l in q:
        low[l], up[l] = shares(q[l], speeds[l])
    for l in range(levels):
        total = centre_of(speeds[l]) * q[l] + low[l + 1][0] + up[l - 1][0]
        total = total + up_row(low[l][1]) + down(up[l][1])
        total = total + jnp.where(rim, inserted(crossing, l), 0.0)
        total = total + jnp.where(lanes >= cols - 1, 0.0, left(low[l][2])) + jnp.where(lanes < 1, 0.0, right(up[l][2]))
        adj_v[l] = total[:rows]

    settle(first + second, 0, send_sem)


def finish(state_v, adj_v, outer, state_hbm, adj_hbm, next_hbm, wide, nxt, out_sem):
    levels, rows, cols = state_v.shape
    flat_rows = levels * rows
    wide_cols = outer.shape[1]
    fine = wide_cols // cols
    outer_rows = outer.shape[0] // levels
    stores = [
        pltpu.make_async_copy(state_v, state_hbm, out_sem.at[0]),
        pltpu.make_async_copy(adj_v, adj_hbm, out_sem.at[1]),
    ]
    for store in stores:
        store.start()
    field = adj_v[...]

    table = (
        lax.broadcasted_iota(jnp.int32, (cols, wide_cols), 0)
        == lax.broadcasted_iota(jnp.int32, (cols, wide_cols), 1) // fine
    ).astype(jnp.float32).astype(jnp.bfloat16)
    halves = bf16_parts(field.reshape(flat_rows, cols), 2)
    spread = jnp.dot(
        jnp.concatenate([h.astype(jnp.bfloat16) for h in halves], axis=1),
        jnp.concatenate([table, table], axis=0),
        preferred_element_type=jnp.float32,
    )
    for k in range(fine):
        for c in range(fine):
            wide[c, pl.ds(k, flat_rows, stride=fine), :] = spread[:, c * cols : (c + 1) * cols]
    for level in range(levels):
        span = pl.ds(level * outer_rows, outer_rows)
        for c in range(fine):
            lanes = pl.ds(c * cols, cols)
            nxt[span, lanes] = (outer[span, lanes].astype(jnp.float32) - wide[c, span, :]).astype(jnp.bfloat16)
        store = pltpu.make_async_copy(nxt.at[span], next_hbm.at[span], out_sem.at[2 + level])
        store.start()
        stores.append(store)
    for store in stores:
        store.wait()


def shards(ends, outer_increment, courant, obs_column, obs_level, obs_value):
    levels, outer_rows, wide_cols = outer_increment.shape
    _, _, rows, cols = courant.shape
    flat_rows = levels * rows
    fine = wide_cols // cols
    lanes = 128
    observed = (obs_column.shape[0] // lanes, lanes)
    span = levels + 4
    assert 4 * levels * GROUP == cols and levels >= REACH and rows % TILE == 0 and ends[1] > 1
    f32, bf16 = jnp.float32, jnp.bfloat16
    outer_shape = (levels * outer_rows, wide_cols)
    vmem = pl.BlockSpec(memory_space=pltpu.VMEM)
    hbm = pl.BlockSpec(memory_space=pl.ANY)
    held = pl.pallas_call(
        functools.partial(kernel, ends),
        out_shape=(
            pltpu.VMEM((levels, rows, cols), f32),
            pltpu.VMEM((levels, rows, cols), f32),
            pltpu.VMEM(outer_shape, bf16),
        ),
        in_specs=[hbm] * 5,
        out_specs=(vmem,) * 3,
        scratch_shapes=[
            pltpu.VMEM(courant.shape, bf16),
            pltpu.VMEM(observed, jnp.int32),
            pltpu.VMEM(observed, jnp.int32),
            pltpu.VMEM(observed, f32),
            pltpu.VMEM((levels * outer_rows, cols), f32),
            pltpu.VMEM((levels, 4, rows, cols), f32),
            pltpu.VMEM((2, REACH - 1, 4, rows, cols), f32),
            pltpu.VMEM((2, rows, cols), f32),
            pltpu.VMEM((2, levels, 4, TILE, cols), f32),
            pltpu.VMEM((2, 2, 2 * TILE, cols), f32),
            pltpu.VMEM((2, 2, 2 * TILE, cols), f32),
            pltpu.VMEM((2, REACH - 1, 4, TILE, cols), f32),
            pltpu.VMEM((rows, cols), f32),
            pltpu.VMEM((3, 3, rows, cols), f32),
            pltpu.VMEM((3, 2, 3, TILE, cols), f32),
            pltpu.VMEM((span, 2, rows, cols), f32),
            pltpu.VMEM((2, span - 2, 2, TILE, cols), f32),
            pltpu.VMEM((2, rows, cols), f32),
            pltpu.VMEM((2, 2, rows, cols), f32),
            pltpu.VMEM((2, 3, 2, TILE, cols), f32),
            pltpu.VMEM((2048, 1, cols), f32),
            pltpu.SemaphoreType.DMA((5,)),
            pltpu.SemaphoreType.DMA,
            pltpu.SemaphoreType.DMA((2,)),
        ],
        compiler_params=pltpu.CompilerParams(collective_id=0, has_side_effects=True),
    )(
        outer_increment.reshape(outer_shape),
        courant,
        obs_column.reshape(observed),
        obs_level.reshape(observed),
        obs_value.reshape(observed),
    )
    state, adjoint, following = pl.pallas_call(
        finish,
        out_shape=(
            jax.ShapeDtypeStruct((levels, rows, cols), f32),
            jax.ShapeDtypeStruct((levels, rows, cols), f32),
            jax.ShapeDtypeStruct(outer_shape, bf16),
        ),
        in_specs=[vmem] * 3,
        out_specs=(hbm,) * 3,
        scratch_shapes=[
            pltpu.VMEM((fine, levels * outer_rows, cols), f32),
            pltpu.VMEM(outer_shape, bf16),
            pltpu.SemaphoreType.DMA((2 + levels,)),
        ],
    )(*[pltpu.with_memory_space_constraint(x, pltpu.VMEM) for x in held])
    return state, adjoint, following.reshape(outer_increment.shape)


def solution(mesh):
    ends = tuple(mesh.shape[a] for a in ("lat", "lon", "lev"))
    block = P("lev", "lat", "lon")
    observed = P(("lat", "lon"))
    return jax.shard_map(
        functools.partial(shards, ends),
        mesh=mesh,
        in_specs=(block, P(None, "lev", "lat", "lon"), observed, observed, observed),
        out_specs=(block, block, block),
        check_vma=False,
    )
```

time: 15.1 us -> 12.3 us (0.81)
  Pallas kernels: 14.3 us -> 11.5 us
    pallas_call x1, Pallas kernels: 13.3 us -> 10.6 us  [shards(): pl.pallas_call(functools.partial(kernel, ends), out_shape=(pltpu.VMEM((le...]
where the time goes in v2:
time: 12.3 us; the launch traced here: 12.2 us
  Pallas kernels  11.5 us (93%)
  between operations  0.64 us (5%)
    pallas_call x1, Pallas kernels, shards(): pl.pallas_call(functools.partial(kernel, ends), out_shape=(pltpu.VMEM((le...  10.6 us
    pallas_call x1, Pallas kernels, shards(): pl.pallas_call(finish, out_shape=(jax.ShapeDtypeStruct((levels, rows, col...  0.94 us

profile of v2, /device:TPU:0, one launch (start us, length us, event | category | flops | bytes accessed | tf_op | source)
XLA Modules:
  0.0 12.2 jit_solution(6039636366079377546)
XLA Ops:
  0.6 10.6 %shard_map.76 = (f32[4,16,128]{2,1,0:T(8,128)S(1)}, f32[4,16,128]{2,1,0:T(8,128)S(1)}, bf16[256,512]{1,0:T(8,128)(2,1)S(1)}) custom-call(bf16[256,512]{1,0:T(8,128)(2,1)} %bitcast.5, bf16[3,4,16,128]{3,2,1,0:T(8,128)(2,1)} %courant_hbm.1, s32[16,128]{1,0:T(8,128)} %bitcast.6, s32[16,128]{1,0:T(8,128)} %bitcast.7, f32[16,128]{1,0:T(8,128)} %bitcast.8), custom_call_target="tpu_custom_call" | custom-call | tf_op jit(solution)/shard_map/pallas_call | solution.py:434
  11.2 0.9 %shard_map.77 = (f32[4,16,128]{2,1,0:T(8,128)}, f32[4,16,128]{2,1,0:T(8,128)}, bf16[256,512]{1,0:T(8,128)(2,1)}) custom-call(f32[4,16,128]{2,1,0:T(8,128)S(1)} %get-tuple-element.9.state_v, f32[4,16,128]{2,1,0:T(8,128)S(1)} %get-tuple-element.10.adj_v, bf16[256,512]{1,0:T(8,128)(2,1)S(1)} %get-tuple-element.11.outer), custom_call_target="tpu_custom_call" | custom-call | tf_op jit(solution)/shard_map/pallas_call | solution.py:477

commit v3 on v2

--- a/solution.py
+++ b/solution.py
@@ -50,7 +50,7 @@
     own, face_in, last_in, side_in, edge_out, edge_in, halo,
     strip, strip_full, strip_half,
     seen, seen_in, seen_strip, seen_full, seen_half, units,
-    in_sem, send_sem, recv_sem,
+    in_sem, send_sem, recv_sem, ready,
 ):
     n_lat, n_lon, n_lev = ends
     levels, rows, cols = state_v.shape
@@ -82,9 +82,17 @@
         else:
             pl.when(exists)(action)
 
+    def stage_of(which):
+        if 0 in which:
+            return 3
+        if 1 in which:
+            return 1 if len(which) == 3 else 0
+        return 2 if 2 in which else 0
+
     class Message:
         def __init__(self, which, source, landing, sem):
             self.needs = tuple(w for w in which if w < 4)
+            self.stage = stage_of(which)
             self.target = {links[w][0]: links[w][1] for w in which}
             self.exists = both([links[w][2] for w in self.needs])
             self.arrives = both([links[w ^ 1][2] for w in self.needs])
@@ -139,13 +147,29 @@
                         second.append(Message(which, seen.at[kept, :, pl.ds(*bands[t])], seen_in.at[t], 1))
     first.sort(key=lambda m: m.lines() - 64 * len(m.target))
 
+    def count(chosen):
+        return sum(
+            1 if flags is None else flags.astype(jnp.int32)
+            for flags in (both([links[w][2] for w in which if w < 4]) for which in chosen)
+        )
+
+    def signal(sem, chosen):
+        for which in chosen:
+            target = {links[w][0]: links[w][1] for w in which}
+            guarded(
+                both([links[w][2] for w in which if w < 4]),
+                lambda target=target: pl.semaphore_signal(sem, inc=1, device_id=target, device_id_type=MESH),
+            )
+
     barrier = pltpu.get_barrier_semaphore()
-    expected = 0
-    for which in partners:
-        exists = both([links[w][2] for w in which if w < 4])
-        target = {links[w][0]: links[w][1] for w in which}
-        guarded(exists, lambda target=target: pl.semaphore_signal(barrier, inc=1, device_id=target, device_id_type=MESH))
-        expected = expected + (1 if exists is None else exists.astype(jnp.int32))
+    near_by = [which for which in partners if len(which) < 3 or not {0, 1} & set(which)]
+    lower = [which for which in near_by if 1 in which]
+    upper = [which for which in near_by if 0 in which]
+    level = [which for which in near_by if which not in lower + upper]
+    north = [which for which in level if 2 in which]
+    south = [which for which in level if 3 in which]
+    around = [which for which in level if which not in north + south]
+    signal(barrier, upper + north + around)
 
     loads = [
         pltpu.make_async_copy(src, dst, in_sem.at[i])
@@ -209,9 +233,13 @@
                 r = rows - j if t == 0 else j - 1
                 edge_out[s, t, n : n + 1, :] = own[l, f, r : r + 1, :]
 
-    pl.semaphore_wait(barrier, expected)
+    pl.semaphore_wait(barrier, count(lower + south + around))
+    signal(ready.at[0], around)
+    signal(ready.at[2], lower)
+    signal(ready.at[1], south)
     for m in first:
-        m.start()
+        if m.stage == 0:
+            m.start()
 
     for load in loads[2:]:
         load.wait()
@@ -246,7 +274,13 @@
             ends_only = jnp.where(group == place, pltpu.roll(values[g], (REACH + GROUP * place) % cols, axis=1), ends_only)
         seen_strip[i] = ends_only
     for m in second:
-        m.start()
+        if m.stage == 0:
+            m.start()
+    for stage, chosen, exists in ((1, around, None), (2, north, links[2][2]), (3, upper, links[0][2])):
+        guarded(exists, lambda stage=stage, chosen=chosen: pl.semaphore_wait(ready.at[stage - 1], count(chosen)))
+        for m in first + second:
+            if m.stage == stage:
+                m.start()
 
     settle(first, 1, recv_sem.at[0])
 
@@ -465,6 +499,7 @@
             pltpu.SemaphoreType.DMA((5,)),
             pltpu.SemaphoreType.DMA,
             pltpu.SemaphoreType.DMA((2,)),
+            pltpu.SemaphoreType.REGULAR((3,)),
         ],
         compiler_params=pltpu.CompilerParams(collective_id=0, has_side_effects=True),
     )(

time: 12.3 us -> 12 us (0.976)
  the two profiles are of different devices: /device:TPU:0 before, /device:TPU:1 now
where the time goes in v3:
time: 12 us; the launch traced here: 11.8 us
  Pallas kernels  11.2 us (93%)
  between operations  0.64 us (5%)
    pallas_call x1, Pallas kernels, shards(): pl.pallas_call(functools.partial(kernel, ends), out_shape=(pltpu.VMEM((le...  10.3 us
    pallas_call x1, Pallas kernels, shards(): pl.pallas_call(finish, out_shape=(jax.ShapeDtypeStruct((levels, rows, col...  0.94 us

profile of v3, /device:TPU:1, one launch (start us, length us, event | category | flops | bytes accessed | tf_op | source)
XLA Modules:
  0.0 11.8 jit_solution(11851240396806741448)
XLA Ops:
  0.6 10.3 %shard_map.76 = (f32[4,16,128]{2,1,0:T(8,128)S(1)}, f32[4,16,128]{2,1,0:T(8,128)S(1)}, bf16[256,512]{1,0:T(8,128)(2,1)S(1)}) custom-call(bf16[256,512]{1,0:T(8,128)(2,1)} %bitcast.5, bf16[3,4,16,128]{3,2,1,0:T(8,128)(2,1)} %courant_hbm.1, s32[16,128]{1,0:T(8,128)} %bitcast.6, s32[16,128]{1,0:T(8,128)} %bitcast.7, f32[16,128]{1,0:T(8,128)} %bitcast.8), custom_call_target="tpu_custom_call" | custom-call | tf_op jit(solution)/shard_map/pallas_call | solution.py:468
  10.9 0.9 %shard_map.77 = (f32[4,16,128]{2,1,0:T(8,128)}, f32[4,16,128]{2,1,0:T(8,128)}, bf16[256,512]{1,0:T(8,128)(2,1)}) custom-call(f32[4,16,128]{2,1,0:T(8,128)S(1)} %get-tuple-element.9.state_v, f32[4,16,128]{2,1,0:T(8,128)S(1)} %get-tuple-element.10.adj_v, bf16[256,512]{1,0:T(8,128)(2,1)S(1)} %get-tuple-element.11.outer), custom_call_target="tpu_custom_call" | custom-call | tf_op jit(solution)/shard_map/pallas_call | solution.py:512

commit v4 on v3

--- a/solution.py
+++ b/solution.py
@@ -47,7 +47,7 @@
     ends, outer_hbm, courant_hbm, col_hbm, lvl_hbm, val_hbm,
     state_v, adj_v, outer,
     courant, col, lvl, val, sums,
-    own, face_in, last_in, side_in, edge_out, edge_in, halo,
+    own, face_in, deep_out, deep_in, side_in, edge_out, edge_in, halo,
     strip, strip_full, strip_half,
     seen, seen_in, seen_strip, seen_full, seen_half, units,
     in_sem, send_sem, recv_sem, ready,
@@ -84,15 +84,15 @@
 
     def stage_of(which):
         if 0 in which:
-            return 3
+            return 3 if len(which) == 1 else 4
         if 1 in which:
             return 1 if len(which) == 3 else 0
         return 2 if 2 in which else 0
 
     class Message:
-        def __init__(self, which, source, landing, sem):
+        def __init__(self, which, source, landing, sem, stage=None):
             self.needs = tuple(w for w in which if w < 4)
-            self.stage = stage_of(which)
+            self.stage = stage_of(which) if stage is None else stage
             self.target = {links[w][0]: links[w][1] for w in which}
             self.exists = both([links[w][2] for w in self.needs])
             self.arrives = both([links[w ^ 1][2] for w in self.needs])
@@ -129,10 +129,9 @@
                     first.append(Message(which, strip.at[pl.ds(*bands[t])], strip_half.at[a, t, b], 0))
                 if u is None:
                     if a and t is None:
-                        begin = levels - near if a == 1 else 0
-                        furthest = levels - REACH if a == 1 else near
-                        first.append(Message(which, own.at[pl.ds(begin, near)], face_in.at[a - 1], 0))
-                        first.append(Message(which, own.at[furthest, 0], last_in.at[a - 1], 0))
+                        begin = levels - near + 1 if a == 1 else 0
+                        first.append(Message(which, own.at[pl.ds(begin, near - 1)], face_in.at[a - 1], 0))
+                        first.append(Message(which, deep_out.at[a - 1], deep_in.at[a - 1], 0, 1 if a == 2 else 4))
                     elif a:
                         first.append(Message(which, edge_out.at[a - 1, t], edge_in.at[a - 1, t], 0))
                     else:
@@ -163,8 +162,8 @@
 
     barrier = pltpu.get_barrier_semaphore()
     near_by = [which for which in partners if len(which) < 3 or not {0, 1} & set(which)]
-    lower = [which for which in near_by if 1 in which]
-    upper = [which for which in near_by if 0 in which]
+    lower = sorted([which for which in near_by if 1 in which], key=len)
+    upper = sorted([which for which in near_by if 0 in which], key=len)
     level = [which for which in near_by if which not in lower + upper]
     north = [which for which in level if 2 in which]
     south = [which for which in level if 3 in which]
@@ -235,11 +234,25 @@
 
     pl.semaphore_wait(barrier, count(lower + south + around))
     signal(ready.at[0], around)
-    signal(ready.at[2], lower)
+    signal(ready.at[2], lower[:1])
+    signal(ready.at[3], lower[1:])
     signal(ready.at[1], south)
     for m in first:
         if m.stage == 0:
             m.start()
+
+    row = lax.broadcasted_iota(jnp.int32, (rows, cols), 0)
+    for s in range(2):
+        l = levels - near if s == 0 else near - 1
+        v = own[l, 0]
+        c = [own[l, k + 1] for k in range(3)]
+        above = jnp.where(row == 0, 0.0, pltpu.roll(v, 1, axis=0))
+        below = jnp.where(row == rows - 1, 0.0, pltpu.roll(v, rows - 1, axis=0))
+        deep_out[s, 0] = v
+        deep_out[s, 1] = forward(
+            v, c, [own[l - 1, 0], above, pltpu.roll(v, 1, axis=1)], [own[l + 1, 0], below, pltpu.roll(v, cols - 1, axis=1)]
+        )
+        deep_out[s, 2] = c[1]
 
     for load in loads[2:]:
         load.wait()
@@ -276,7 +289,7 @@
     for m in second:
         if m.stage == 0:
             m.start()
-    for stage, chosen, exists in ((1, around, None), (2, north, links[2][2]), (3, upper, links[0][2])):
+    for stage, chosen, exists in ((1, around, None), (2, north, links[2][2]), (3, upper[:1], links[0][2]), (4, upper[1:], links[0][2])):
         guarded(exists, lambda stage=stage, chosen=chosen: pl.semaphore_wait(ready.at[stage - 1], count(chosen)))
         for m in first + second:
             if m.stage == stage:
@@ -304,9 +317,9 @@
         if 0 <= l < levels:
             return joined(own[l, f], side_in[0, l, f], side_in[1, l, f])
         s, i = (0, -l) if l < 0 else (1, l - levels + 1)
-        if i == REACH:
-            return jnp.concatenate([last_in[s], blank], axis=0)
-        full = face_in[s, near - i, f] if s == 0 else face_in[s, i - 1, f]
+        if i == near:
+            return jnp.concatenate([deep_in[s, f], halo[s, i - 1, f]], axis=0)
+        full = face_in[s, near - 1 - i, f] if s == 0 else face_in[s, i - 1, f]
         return jnp.concatenate([full, halo[s, i - 1, f]], axis=0)
 
     def down(x):
@@ -348,13 +361,20 @@
     def inserted(z, l):
         return right(z, (cols - REACH - GROUP * (l + REACH)) % cols)
 
-    speeds = {l: [cell(l, k + 1) for k in range(3)] for l in range(-near, levels + near)}
-    v = {l: cell(l, 0) for l in range(-REACH, levels + REACH)}
-    for reach in (near, near - 1):
-        v = {
-            l: forward(v[l], speeds[l], [v[l - 1], down(v[l]), right(v[l])], [v[l + 1], up_row(v[l]), left(v[l])])
-            for l in range(-reach, levels + reach)
-        }
+    speeds = {l: [cell(l, k + 1) for k in range(3)] for l in range(1 - near, levels + near - 1)}
+    start = {l: cell(l, 0) for l in range(-near, levels + near)}
+
+    def step(v, l):
+        return forward(v[l], speeds[l], [v[l - 1], down(v[l]), right(v[l])], [v[l + 1], up_row(v[l]), left(v[l])])
+
+    v = {l: step(start, l) for l in speeds}
+    for s in range(2):
+        l = -near if s == 0 else levels + near - 1
+        c = deep_in[s, 2]
+        above = jnp.where((row == 0) & (c > 0.0), down(start[l])[:rows], 0.0)
+        below = jnp.where((row == rows - 1) & (c <= 0.0), up_row(start[l])[:rows], 0.0)
+        v[l] = jnp.concatenate([deep_in[s, 1] + jnp.abs(c) * (above + below), blank], axis=0)
+    v = {l: step(v, l) for l in speeds}
     fix = jnp.where(left_half, side_v[1], side_v[0])
     rim = (lanes < 2) | (lanes >= cols - 2)
     v = {l: jnp.where(rim, inserted(fix, l), v[l]) for l in v}
@@ -481,8 +501,9 @@
             pltpu.VMEM(observed, f32),
             pltpu.VMEM((levels * outer_rows, cols), f32),
             pltpu.VMEM((levels, 4, rows, cols), f32),
-            pltpu.VMEM((2, REACH - 1, 4, rows, cols), f32),
-            pltpu.VMEM((2, rows, cols), f32),
+            pltpu.VMEM((2, REACH - 2, 4, rows, cols), f32),
+            pltpu.VMEM((2, 3, rows, cols), f32),
+            pltpu.VMEM((2, 3, rows, cols), f32),
             pltpu.VMEM((2, levels, 4, TILE, cols), f32),
             pltpu.VMEM((2, 2, 2 * TILE, cols), f32),
             pltpu.VMEM((2, 2, 2 * TILE, cols), f32),
@@ -499,7 +520,7 @@
             pltpu.SemaphoreType.DMA((5,)),
             pltpu.SemaphoreType.DMA,
             pltpu.SemaphoreType.DMA((2,)),
-            pltpu.SemaphoreType.REGULAR((3,)),
+            pltpu.SemaphoreType.REGULAR((4,)),
         ],
         compiler_params=pltpu.CompilerParams(collective_id=0, has_side_effects=True),
     )(

time: 12 us -> 11.4 us (0.950)
  Pallas kernels: 11.2 us -> 10.6 us
    pallas_call x1, Pallas kernels: 10.3 us -> 9.64 us  [shards(): pl.pallas_call(functools.partial(kernel, ends), out_shape=(pltpu.VMEM((le...]
where the time goes in v4:
time: 11.4 us; the launch traced here: 11.2 us
  Pallas kernels  10.6 us (93%)
  between operations  0.64 us (6%)
    pallas_call x1, Pallas kernels, shards(): pl.pallas_call(functools.partial(kernel, ends), out_shape=(pltpu.VMEM((le...  9.64 us
    pallas_call x1, Pallas kernels, shards(): pl.pallas_call(finish, out_shape=(jax.ShapeDtypeStruct((levels, rows, col...  0.94 us

profile of v4, /device:TPU:1, one launch (start us, length us, event | category | flops | bytes accessed | tf_op | source)
XLA Modules:
  0.0 11.2 jit_solution(16026050837855011734)
XLA Ops:
  0.6 9.6 %shard_map.76 = (f32[4,16,128]{2,1,0:T(8,128)S(1)}, f32[4,16,128]{2,1,0:T(8,128)S(1)}, bf16[256,512]{1,0:T(8,128)(2,1)S(1)}) custom-call(bf16[256,512]{1,0:T(8,128)(2,1)} %bitcast.5, bf16[3,4,16,128]{3,2,1,0:T(8,128)(2,1)} %courant_hbm.1, s32[16,128]{1,0:T(8,128)} %bitcast.6, s32[16,128]{1,0:T(8,128)} %bitcast.7, f32[16,128]{1,0:T(8,128)} %bitcast.8), custom_call_target="tpu_custom_call" | custom-call | tf_op jit(solution)/shard_map/pallas_call | solution.py:488
  10.3 0.9 %shard_map.77 = (f32[4,16,128]{2,1,0:T(8,128)}, f32[4,16,128]{2,1,0:T(8,128)}, bf16[256,512]{1,0:T(8,128)(2,1)}) custom-call(f32[4,16,128]{2,1,0:T(8,128)S(1)} %get-tuple-element.9.state_v, f32[4,16,128]{2,1,0:T(8,128)S(1)} %get-tuple-element.10.adj_v, bf16[256,512]{1,0:T(8,128)(2,1)S(1)} %get-tuple-element.11.outer), custom_call_target="tpu_custom_call" | custom-call | tf_op jit(solution)/shard_map/pallas_call | solution.py:533

commit v5 on v4

--- a/solution.py
+++ b/solution.py
@@ -61,6 +61,15 @@
     span = seen.shape[0]
     beyond = (span - levels) // 2
 
+    loads = [
+        pltpu.make_async_copy(src, dst, in_sem.at[i])
+        for i, (src, dst) in enumerate(
+            ((outer_hbm, outer), (courant_hbm, courant), (col_hbm, col), (lvl_hbm, lvl), (val_hbm, val))
+        )
+    ]
+    for load in loads:
+        load.start()
+
     me_lat, me_lon, me_lev = (lax.axis_index(a) for a in ("lat", "lon", "lev"))
     links = (
         ("lev", me_lev + 1, me_lev < n_lev - 1),
@@ -82,30 +91,34 @@
         else:
             pl.when(exists)(action)
 
-    def stage_of(which):
-        if 0 in which:
-            return 3 if len(which) == 1 else 4
-        if 1 in which:
-            return 1 if len(which) == 3 else 0
-        return 2 if 2 in which else 0
+    def flags_of(which):
+        return [links[w][2] for w in which if w < 4]
+
+    def lon_of(which):
+        return [w for w in which if w > 3]
+
+    def is_ahead(which):
+        return me_lon < links[lon_of(which)[0]][1]
+
+    def is_behind(which):
+        return me_lon > links[lon_of(which)[0]][1]
 
     class Message:
-        def __init__(self, which, source, landing, sem, stage=None):
+        def __init__(self, which, source, landing, sem, later=False):
+            self.which, self.later = which, later
             self.needs = tuple(w for w in which if w < 4)
-            self.stage = stage_of(which) if stage is None else stage
             self.target = {links[w][0]: links[w][1] for w in which}
-            self.exists = both([links[w][2] for w in self.needs])
             self.arrives = both([links[w ^ 1][2] for w in self.needs])
             self.source, self.landing, self.sem = source, landing, sem
 
-        def start(self):
+        def start(self, flag=None):
             def begin():
                 pltpu.make_async_remote_copy(
                     src_ref=self.source, dst_ref=self.landing, send_sem=send_sem, recv_sem=recv_sem.at[self.sem],
                     device_id=self.target, device_id_type=MESH,
                 ).start()
 
-            guarded(self.exists, begin)
+            guarded(both(flags_of(self.which) + ([] if flag is None else [flag])), begin)
 
         def lines(self):
             total = 1
@@ -113,7 +126,7 @@
                 total = total * n
             return total // cols
 
-    partners, first, second = [], [], []
+    partners, first, second, faces = [], [], [], []
     for a in (2, 1, 0):
         for t in (0, 1, None):
             for u in turns + (None,):
@@ -129,13 +142,14 @@
                     first.append(Message(which, strip.at[pl.ds(*bands[t])], strip_half.at[a, t, b], 0))
                 if u is None:
                     if a and t is None:
-                        begin = levels - near + 1 if a == 1 else 0
-                        first.append(Message(which, own.at[pl.ds(begin, near - 1)], face_in.at[a - 1], 0))
-                        first.append(Message(which, deep_out.at[a - 1], deep_in.at[a - 1], 0, 1 if a == 2 else 4))
+                        for i in range(1, near):
+                            l, place = (levels - i, near - 1 - i) if a == 1 else (i - 1, i - 1)
+                            faces.append(Message(which, own.at[l], face_in.at[a - 1, place], 2, i > 1))
+                        faces.append(Message(which, deep_out.at[a - 1], deep_in.at[a - 1], 2, True))
                     elif a:
                         first.append(Message(which, edge_out.at[a - 1, t], edge_in.at[a - 1, t], 0))
                     else:
-                        first.append(Message(which, own.at[:, :, pl.ds(*bands[t])], side_in.at[t], 0))
+                        faces.append(Message(which, own.at[:, :, pl.ds(*bands[t])], side_in.at[t], 2))
                 if not a:
                     if t is None:
                         second.append(Message(which, seen_strip, seen_full.at[u], 1))
@@ -144,40 +158,43 @@
                     if u is None:
                         kept = pl.ds(1, span - 2)
                         second.append(Message(which, seen.at[kept, :, pl.ds(*bands[t])], seen_in.at[t], 1))
-    first.sort(key=lambda m: m.lines() - 64 * len(m.target))
+    first.sort(key=lambda m: -len(m.target))
+
+    def pick(test, side=None):
+        return [(which, None if side is None else side(which)) for which in partners if test(which)]
 
     def count(chosen):
-        return sum(
-            1 if flags is None else flags.astype(jnp.int32)
-            for flags in (both([links[w][2] for w in which if w < 4]) for which in chosen)
-        )
+        total = 0
+        for which, flag in chosen:
+            exists = both(flags_of(which) + ([] if flag is None else [flag]))
+            total = total + (1 if exists is None else exists.astype(jnp.int32))
+        return total
 
     def signal(sem, chosen):
-        for which in chosen:
+        for which, flag in chosen:
             target = {links[w][0]: links[w][1] for w in which}
             guarded(
-                both([links[w][2] for w in which if w < 4]),
+                both(flags_of(which) + ([] if flag is None else [flag])),
                 lambda target=target: pl.semaphore_signal(sem, inc=1, device_id=target, device_id_type=MESH),
             )
 
+    def level_lon(which):
+        return lon_of(which) and not {0, 1} & set(which)
+
+    def corner(which):
+        return len(which) == 3
+
+    lower = pick(lambda w: 1 in w and not corner(w))
+    upper = pick(lambda w: 0 in w and not corner(w))
+    lower_face, upper_face = [[c for c in side if len(c[0]) == 1] for side in (lower, upper)]
+    lower_rest, upper_rest = [[c for c in side if len(c[0]) > 1] for side in (lower, upper)]
+    lower_south = pick(lambda w: corner(w) and 1 in w and 3 in w)
+    upper_north = pick(lambda w: corner(w) and 0 in w and 2 in w)
+    south, north = pick(lambda w: w == [3]), pick(lambda w: w == [2])
+    behind, ahead = pick(level_lon, is_behind), pick(level_lon, is_ahead)
+
     barrier = pltpu.get_barrier_semaphore()
-    near_by = [which for which in partners if len(which) < 3 or not {0, 1} & set(which)]
-    lower = sorted([which for which in near_by if 1 in which], key=len)
-    upper = sorted([which for which in near_by if 0 in which], key=len)
-    level = [which for which in near_by if which not in lower + upper]
-    north = [which for which in level if 2 in which]
-    south = [which for which in level if 3 in which]
-    around = [which for which in level if which not in north + south]
-    signal(barrier, upper + north + around)
-
-    loads = [
-        pltpu.make_async_copy(src, dst, in_sem.at[i])
-        for i, (src, dst) in enumerate(
-            ((outer_hbm, outer), (courant_hbm, courant), (col_hbm, col), (lvl_hbm, lvl), (val_hbm, val))
-        )
-    ]
-    for load in loads:
-        load.start()
+    signal(barrier, upper_north + upper_rest + upper_face + ahead + north)
 
     def settle(messages, flip, sem, known=()):
         if len(known) < 4:
@@ -194,7 +211,7 @@
     def clear(ref):
         ref[...] = jnp.zeros(ref.shape, jnp.float32)
 
-    for m in first + second:
+    for m in first + second + faces:
         if m.arrives is not None:
             pl.when(jnp.logical_not(m.arrives))(lambda m=m: clear(m.landing))
     clear(halo)
@@ -232,14 +249,27 @@
                 r = rows - j if t == 0 else j - 1
                 edge_out[s, t, n : n + 1, :] = own[l, f, r : r + 1, :]
 
-    pl.semaphore_wait(barrier, count(lower + south + around))
-    signal(ready.at[0], around)
-    signal(ready.at[2], lower[:1])
-    signal(ready.at[3], lower[1:])
+    def send(messages, test, side=None, later=False):
+        for m in messages:
+            if test(m.which) and m.later == later:
+                m.start(None if side is None else side(m.which))
+
+    def at_once(w):
+        return (1 in w and not (corner(w) and 2 in w)) or w == [3]
+
+    def to_north(w):
+        return w == [2] or (corner(w) and 1 in w and 2 in w)
+
+    expected = count(lower + lower_south + south + behind)
+    pl.when(expected > 0)(lambda: pl.semaphore_wait(barrier, expected))
+    signal(ready.at[3], lower_rest)
+    signal(ready.at[0], behind)
+    signal(ready.at[2], lower_face)
     signal(ready.at[1], south)
-    for m in first:
-        if m.stage == 0:
-            m.start()
+    signal(ready.at[4], [(w, is_behind(w)) for w, _ in lower_south])
+    send(first, at_once)
+    send(first, level_lon, is_behind)
+    send(faces, at_once)
 
     row = lax.broadcasted_iota(jnp.int32, (rows, cols), 0)
     for s in range(2):
@@ -286,16 +316,39 @@
             place = g + REACH - beyond
             ends_only = jnp.where(group == place, pltpu.roll(values[g], (REACH + GROUP * place) % cols, axis=1), ends_only)
         seen_strip[i] = ends_only
-    for m in second:
-        if m.stage == 0:
-            m.start()
-    for stage, chosen, exists in ((1, around, None), (2, north, links[2][2]), (3, upper[:1], links[0][2]), (4, upper[1:], links[0][2])):
-        guarded(exists, lambda stage=stage, chosen=chosen: pl.semaphore_wait(ready.at[stage - 1], count(chosen)))
-        for m in first + second:
-            if m.stage == stage:
-                m.start()
+    send(second, at_once)
+    send(second, level_lon, is_behind)
+
+    def go_north():
+        pl.semaphore_wait(ready.at[1], 1)
+        send(first + faces + second, to_north)
+
+    early = me_lon > 0
+    pl.when(links[2][2] & early)(go_north)
+    send(faces, at_once, later=True)
+    pl.when(links[2][2] & jnp.logical_not(early))(go_north)
+
+    @pl.when(me_lon < n_lon - 1)
+    def _():
+        pl.semaphore_wait(ready.at[0], count(ahead))
+        send(first + second, level_lon, is_ahead)
+
+    @pl.when(links[0][2])
+    def _():
+        pl.semaphore_wait(ready.at[2], 1)
+        send(faces, lambda w: 0 in w)
+        pl.semaphore_wait(ready.at[3], count(upper_rest))
+        send(first, lambda w: 0 in w and not (corner(w) and 2 in w))
+        send(first, lambda w: corner(w) and 0 in w and 2 in w, is_behind)
+        send(faces, lambda w: 0 in w, later=True)
+
+    @pl.when(links[0][2] & links[2][2] & (me_lon < n_lon - 1))
+    def _():
+        pl.semaphore_wait(ready.at[4], count([(w, is_ahead(w)) for w, _ in upper_north]))
+        send(first, lambda w: corner(w) and 0 in w and 2 in w, is_ahead)
 
     settle(first, 1, recv_sem.at[0])
+    settle(second, 1, recv_sem.at[1])
 
     tall = rows + TILE
     half = lax.broadcasted_iota(jnp.int32, (TILE, cols), 0) < TILE // 2
@@ -360,34 +413,6 @@
 
     def inserted(z, l):
         return right(z, (cols - REACH - GROUP * (l + REACH)) % cols)
-
-    speeds = {l: [cell(l, k + 1) for k in range(3)] for l in range(1 - near, levels + near - 1)}
-    start = {l: cell(l, 0) for l in range(-near, levels + near)}
-
-    def step(v, l):
-        return forward(v[l], speeds[l], [v[l - 1], down(v[l]), right(v[l])], [v[l + 1], up_row(v[l]), left(v[l])])
-
-    v = {l: step(start, l) for l in speeds}
-    for s in range(2):
-        l = -near if s == 0 else levels + near - 1
-        c = deep_in[s, 2]
-        above = jnp.where((row == 0) & (c > 0.0), down(start[l])[:rows], 0.0)
-        below = jnp.where((row == rows - 1) & (c <= 0.0), up_row(start[l])[:rows], 0.0)
-        v[l] = jnp.concatenate([deep_in[s, 1] + jnp.abs(c) * (above + below), blank], axis=0)
-    v = {l: step(v, l) for l in speeds}
-    fix = jnp.where(left_half, side_v[1], side_v[0])
-    rim = (lanes < 2) | (lanes >= cols - 2)
-    v = {l: jnp.where(rim, inserted(fix, l), v[l]) for l in v}
-    for l in range(levels):
-        state_v[l] = v[l][:rows]
-
-    settle(second, 1, recv_sem.at[1])
-
-    def seen_cell(l, i):
-        g = l + beyond
-        if 0 < g < span - 1:
-            return joined(seen[g, i], seen_in[0, g - 1, i], seen_in[1, g - 1, i])
-        return jnp.concatenate([seen[g, i], blank], axis=0)
 
     def seen_block(b, i):
         full = seen_strip[i] if b == 0 else seen_full[b - 1, i]
@@ -411,6 +436,38 @@
     fix = jnp.where(left_half, side_q[1][0], side_q[0][0])
     crossing = jnp.where(left_half, side_q[1][1], side_q[0][1])
 
+    fix_v = jnp.where(left_half, side_v[1], side_v[0])
+    fix_v = {l: inserted(fix_v, l) for l in range(2 - near - 1, levels + near - 1)}
+    fix_q = {l: inserted(fix, l) for l in range(-1, levels + 1)}
+    crossing = {l: inserted(crossing, l) for l in range(levels)}
+
+    settle(faces, 1, recv_sem.at[2])
+
+    speeds = {l: [cell(l, k + 1) for k in range(3)] for l in range(1 - near, levels + near - 1)}
+    start = {l: cell(l, 0) for l in range(-near, levels + near)}
+
+    def step(v, l):
+        return forward(v[l], speeds[l], [v[l - 1], down(v[l]), right(v[l])], [v[l + 1], up_row(v[l]), left(v[l])])
+
+    v = {l: step(start, l) for l in speeds}
+    for s in range(2):
+        l = -near if s == 0 else levels + near - 1
+        c = deep_in[s, 2]
+        above = jnp.where((row == 0) & (c > 0.0), down(start[l])[:rows], 0.0)
+        below = jnp.where((row == rows - 1) & (c <= 0.0), up_row(start[l])[:rows], 0.0)
+        v[l] = jnp.concatenate([deep_in[s, 1] + jnp.abs(c) * (above + below), blank], axis=0)
+    v = {l: step(v, l) for l in speeds}
+    rim = (lanes < 2) | (lanes >= cols - 2)
+    v = {l: jnp.where(rim, fix_v[l], v[l]) for l in v}
+    for l in range(levels):
+        state_v[l] = v[l][:rows]
+
+    def seen_cell(l, i):
+        g = l + beyond
+        if 0 < g < span - 1:
+            return joined(seen[g, i], seen_in[0, g - 1, i], seen_in[1, g - 1, i])
+        return jnp.concatenate([seen[g, i], blank], axis=0)
+
     p = {l: seen_cell(l, 0) * v[l] - seen_cell(l, 1) for l in v}
     low, up = {}, {}
     for l in p:
@@ -420,17 +477,17 @@
     for l in range(-1, levels + 1):
         total = centre_of(speeds[l]) * p[l] + low[l + 1][0] + up[l - 1][0]
         total = total + up_row(low[l][1]) + down(up[l][1]) + left(low[l][2]) + right(up[l][2])
-        q[l] = jnp.where(rim, inserted(fix, l), total)
+        q[l] = jnp.where(rim, fix_q[l], total)
     for l in q:
         low[l], up[l] = shares(q[l], speeds[l])
     for l in range(levels):
         total = centre_of(speeds[l]) * q[l] + low[l + 1][0] + up[l - 1][0]
         total = total + up_row(low[l][1]) + down(up[l][1])
-        total = total + jnp.where(rim, inserted(crossing, l), 0.0)
+        total = total + jnp.where(rim, crossing[l], 0.0)
         total = total + jnp.where(lanes >= cols - 1, 0.0, left(low[l][2])) + jnp.where(lanes < 1, 0.0, right(up[l][2]))
         adj_v[l] = total[:rows]
 
-    settle(first + second, 0, send_sem)
+    settle(first + second + faces, 0, send_sem)
 
 
 def finish(state_v, adj_v, outer, state_hbm, adj_hbm, next_hbm, wide, nxt, out_sem):
@@ -519,8 +576,8 @@
             pltpu.VMEM((2048, 1, cols), f32),
             pltpu.SemaphoreType.DMA((5,)),
             pltpu.SemaphoreType.DMA,
-            pltpu.SemaphoreType.DMA((2,)),
-            pltpu.SemaphoreType.REGULAR((4,)),
+            pltpu.SemaphoreType.DMA((3,)),
+            pltpu.SemaphoreType.REGULAR((5,)),
         ],
         compiler_params=pltpu.CompilerParams(collective_id=0, has_side_effects=True),
     )(

time: 11.4 us -> 10.5 us (0.921)
  the two profiles are of different devices: /device:TPU:1 before, /device:TPU:0 now
where the time goes in v5:
time: 10.5 us; the launch traced here: 10.3 us
  Pallas kernels  9.65 us (92%)
  between operations  0.64 us (6%)
    pallas_call x1, Pallas kernels, shards(): pl.pallas_call(functools.partial(kernel, ends), out_shape=(pltpu.VMEM((le...  8.71 us
    pallas_call x1, Pallas kernels, shards(): pl.pallas_call(finish, out_shape=(jax.ShapeDtypeStruct((levels, rows, col...  0.94 us

profile of v5, /device:TPU:0, one launch (start us, length us, event | category | flops | bytes accessed | tf_op | source)
XLA Modules:
  0.0 10.3 jit_solution(440061407333637785)
XLA Ops:
  0.6 8.7 %shard_map.76 = (f32[4,16,128]{2,1,0:T(8,128)S(1)}, f32[4,16,128]{2,1,0:T(8,128)S(1)}, bf16[256,512]{1,0:T(8,128)(2,1)S(1)}) custom-call(bf16[256,512]{1,0:T(8,128)(2,1)} %bitcast.5, bf16[3,4,16,128]{3,2,1,0:T(8,128)(2,1)} %courant_hbm.1, s32[16,128]{1,0:T(8,128)} %bitcast.6, s32[16,128]{1,0:T(8,128)} %bitcast.7, f32[16,128]{1,0:T(8,128)} %bitcast.8), custom_call_target="tpu_custom_call" | custom-call | tf_op jit(solution)/shard_map/pallas_call | solution.py:545
  9.4 0.9 %shard_map.77 = (f32[4,16,128]{2,1,0:T(8,128)}, f32[4,16,128]{2,1,0:T(8,128)}, bf16[256,512]{1,0:T(8,128)(2,1)}) custom-call(f32[4,16,128]{2,1,0:T(8,128)S(1)} %get-tuple-element.9.state_v, f32[4,16,128]{2,1,0:T(8,128)S(1)} %get-tuple-element.10.adj_v, bf16[256,512]{1,0:T(8,128)(2,1)S(1)} %get-tuple-element.11.outer), custom_call_target="tpu_custom_call" | custom-call | tf_op jit(solution)/shard_map/pallas_call | solution.py:590

commit v6 on v5

--- a/solution.py
+++ b/solution.py
@@ -104,7 +104,7 @@
         return me_lon > links[lon_of(which)[0]][1]
 
     class Message:
-        def __init__(self, which, source, landing, sem, later=False):
+        def __init__(self, which, source, landing, sem, later=0):
             self.which, self.later = which, later
             self.needs = tuple(w for w in which if w < 4)
             self.target = {links[w][0]: links[w][1] for w in which}
@@ -142,10 +142,8 @@
                     first.append(Message(which, strip.at[pl.ds(*bands[t])], strip_half.at[a, t, b], 0))
                 if u is None:
                     if a and t is None:
-                        for i in range(1, near):
-                            l, place = (levels - i, near - 1 - i) if a == 1 else (i - 1, i - 1)
-                            faces.append(Message(which, own.at[l], face_in.at[a - 1, place], 2, i > 1))
-                        faces.append(Message(which, deep_out.at[a - 1], deep_in.at[a - 1], 2, True))
+                        faces.append(Message(which, own.at[levels - 1 if a == 1 else 0], face_in.at[a - 1], 2))
+                        faces.append(Message(which, deep_out.at[a - 1], deep_in.at[a - 1], 2, 2))
                     elif a:
                         first.append(Message(which, edge_out.at[a - 1, t], edge_in.at[a - 1, t], 0))
                     else:
@@ -249,7 +247,7 @@
                 r = rows - j if t == 0 else j - 1
                 edge_out[s, t, n : n + 1, :] = own[l, f, r : r + 1, :]
 
-    def send(messages, test, side=None, later=False):
+    def send(messages, test, side=None, later=0):
         for m in messages:
             if test(m.which) and m.later == later:
                 m.start(None if side is None else side(m.which))
@@ -262,27 +260,40 @@
 
     expected = count(lower + lower_south + south + behind)
     pl.when(expected > 0)(lambda: pl.semaphore_wait(barrier, expected))
+    signal(ready.at[4], [(w, is_behind(w)) for w, _ in lower_south])
     signal(ready.at[3], lower_rest)
     signal(ready.at[0], behind)
     signal(ready.at[2], lower_face)
     signal(ready.at[1], south)
-    signal(ready.at[4], [(w, is_behind(w)) for w, _ in lower_south])
     send(first, at_once)
     send(first, level_lon, is_behind)
     send(faces, at_once)
 
     row = lax.broadcasted_iota(jnp.int32, (rows, cols), 0)
-    for s in range(2):
-        l = levels - near if s == 0 else near - 1
-        v = own[l, 0]
-        c = [own[l, k + 1] for k in range(3)]
+    high = rows // TILE
+    zero = jnp.zeros((rows, cols), jnp.float32)
+
+    def inner(v, c, before, after):
         above = jnp.where(row == 0, 0.0, pltpu.roll(v, 1, axis=0))
         below = jnp.where(row == rows - 1, 0.0, pltpu.roll(v, rows - 1, axis=0))
-        deep_out[s, 0] = v
-        deep_out[s, 1] = forward(
-            v, c, [own[l - 1, 0], above, pltpu.roll(v, 1, axis=1)], [own[l + 1, 0], below, pltpu.roll(v, cols - 1, axis=1)]
-        )
-        deep_out[s, 2] = c[1]
+        return forward(v, c, [before, above, pltpu.roll(v, 1, axis=1)], [after, below, pltpu.roll(v, cols - 1, axis=1)])
+
+    def rim_rows(second_level, third_level):
+        kept = [(second_level, 2, r) for r in (0, 1, rows - 2, rows - 1)]
+        return kept + [(second_level, 3, r) for r in (0, rows - 1)] + [(third_level, 2, r) for r in (0, rows - 1)]
+
+    pairs = ((levels - 2, levels - 3), (1, 2))
+    once = {
+        l: inner(own[l, 0], [own[l, k + 1] for k in range(3)], own[l - 1, 0], own[l + 1, 0])
+        for l in sorted(set(pairs[0] + pairs[1]))
+    }
+    for s, (l, far) in enumerate(pairs):
+        c = [own[l, k + 1] for k in range(3)]
+        twice = inner(once[l], c, zero if s else once[far], once[far] if s else zero)
+        for n, plane in enumerate((own[l, 0], once[l], twice, c[0])):
+            deep_out[s, n * high : (n + 1) * high] = plane.reshape(high, TILE, cols)
+        for n, (at, f, r) in enumerate(rim_rows(l, far)):
+            deep_out[s, 4 * high, n : n + 1, :] = own[at, f, r : r + 1, :]
 
     for load in loads[2:]:
         load.wait()
@@ -325,7 +336,7 @@
 
     early = me_lon > 0
     pl.when(links[2][2] & early)(go_north)
-    send(faces, at_once, later=True)
+    send(faces, at_once, later=2)
     pl.when(links[2][2] & jnp.logical_not(early))(go_north)
 
     @pl.when(me_lon < n_lon - 1)
@@ -340,15 +351,15 @@
         pl.semaphore_wait(ready.at[3], count(upper_rest))
         send(first, lambda w: 0 in w and not (corner(w) and 2 in w))
         send(first, lambda w: corner(w) and 0 in w and 2 in w, is_behind)
-        send(faces, lambda w: 0 in w, later=True)
 
     @pl.when(links[0][2] & links[2][2] & (me_lon < n_lon - 1))
     def _():
         pl.semaphore_wait(ready.at[4], count([(w, is_ahead(w)) for w, _ in upper_north]))
         send(first, lambda w: corner(w) and 0 in w and 2 in w, is_ahead)
 
+    pl.when(links[0][2])(lambda: send(faces, lambda w: 0 in w, later=2))
+
     settle(first, 1, recv_sem.at[0])
-    settle(second, 1, recv_sem.at[1])
 
     tall = rows + TILE
     half = lax.broadcasted_iota(jnp.int32, (TILE, cols), 0) < TILE // 2
@@ -370,10 +381,7 @@
         if 0 <= l < levels:
             return joined(own[l, f], side_in[0, l, f], side_in[1, l, f])
         s, i = (0, -l) if l < 0 else (1, l - levels + 1)
-        if i == near:
-            return jnp.concatenate([deep_in[s, f], halo[s, i - 1, f]], axis=0)
-        full = face_in[s, near - 1 - i, f] if s == 0 else face_in[s, i - 1, f]
-        return jnp.concatenate([full, halo[s, i - 1, f]], axis=0)
+        return jnp.concatenate([face_in[s, f], halo[s, i - 1, f]], axis=0)
 
     def down(x):
         return pltpu.roll(x, 1, axis=0)
@@ -418,6 +426,7 @@
         full = seen_strip[i] if b == 0 else seen_full[b - 1, i]
         return joined(full, seen_half[0, b, i], seen_half[1, b, i])
 
+    settle(second, 1, recv_sem.at[1])
     side_q = []
     for side in range(2):
         known = []
@@ -443,20 +452,58 @@
 
     settle(faces, 1, recv_sem.at[2])
 
-    speeds = {l: [cell(l, k + 1) for k in range(3)] for l in range(1 - near, levels + near - 1)}
-    start = {l: cell(l, 0) for l in range(-near, levels + near)}
+    speeds = {l: [cell(l, k + 1) for k in range(3)] for l in range(-1, levels + 1)}
+    start = {l: cell(l, 0) for l in range(-1, levels + 1)}
+    beside = ((-2, -1, -3), (levels + 1, levels, levels + 2))
+
+    def deep(s, n):
+        return deep_in[s, n * high : (n + 1) * high].reshape(rows, cols)
+
+    def kept_rows(s, places):
+        plane = zero
+        for n, r in places:
+            plane = jnp.where(row == r, deep_in[s, 4 * high, n : n + 1, :], plane)
+        return plane
+
+    def across(c, x):
+        above = jnp.where((row == 0) & (c > 0.0), down(x)[:rows], 0.0)
+        below = jnp.where((row == rows - 1) & (c <= 0.0), up_row(x)[:rows], 0.0)
+        return jnp.abs(c) * (above + below)
 
     def step(v, l):
         return forward(v[l], speeds[l], [v[l - 1], down(v[l]), right(v[l])], [v[l + 1], up_row(v[l]), left(v[l])])
 
-    v = {l: step(start, l) for l in speeds}
-    for s in range(2):
-        l = -near if s == 0 else levels + near - 1
-        c = deep_in[s, 2]
-        above = jnp.where((row == 0) & (c > 0.0), down(start[l])[:rows], 0.0)
-        below = jnp.where((row == rows - 1) & (c <= 0.0), up_row(start[l])[:rows], 0.0)
-        v[l] = jnp.concatenate([deep_in[s, 1] + jnp.abs(c) * (above + below), blank], axis=0)
-    v = {l: step(v, l) for l in speeds}
+    outside = []
+    for s, (l, _, far) in enumerate(beside):
+        c = [
+            deep(s, 3),
+            kept_rows(s, ((0, 0), (1, 1), (2, rows - 2), (3, rows - 1))),
+            kept_rows(s, ((4, 0), (5, rows - 1))),
+        ]
+        start[l] = jnp.concatenate([deep(s, 0), halo[s, 1, 0]], axis=0)
+        start[far] = jnp.concatenate([zero, halo[s, 2, 0]], axis=0)
+        speeds[l] = [jnp.concatenate([c[k], halo[s, 1, k + 1]], axis=0) for k in range(3)]
+        gained = across(c[1], start[l])
+        further = across(kept_rows(s, ((6, 0), (7, rows - 1))), start[far])
+        outside.append((c, gained, further))
+    v = {l: step(start, l) for l in range(-1, levels + 1)}
+    for s, (l, _, _) in enumerate(beside):
+        v[l] = jnp.concatenate([deep(s, 1) + outside[s][1], step(start, l)[rows:]], axis=0)
+    second_v = {l: step(v, l) for l in range(-1, levels + 1)}
+    for s, (l, by, _) in enumerate(beside):
+        c, gained, further = outside[s]
+        sizes = [jnp.abs(n) for n in c]
+        inward, outward = v[by][:rows], further
+        crossed = jnp.concatenate([gained, v[l][rows:]], axis=0)
+        total = deep(s, 2) + (1.0 - sizes[0] - sizes[1] - sizes[2]) * gained
+        total = total + sizes[0] * jnp.where(c[0] > 0.0, inward if s else outward, outward if s else inward)
+        total = total + sizes[1] * jnp.where(c[1] > 0.0, down(crossed)[:rows], up_row(crossed)[:rows])
+        total = total + sizes[2] * jnp.where(
+            c[2] > 0.0, pltpu.roll(gained, 1, axis=1), pltpu.roll(gained, cols - 1, axis=1)
+        )
+        second_v[l] = jnp.concatenate([total, blank], axis=0)
+        speeds[l] = [jnp.concatenate([c[0], blank], axis=0)]
+    v = second_v
     rim = (lanes < 2) | (lanes >= cols - 2)
     v = {l: jnp.where(rim, fix_v[l], v[l]) for l in v}
     for l in range(levels):
@@ -558,9 +605,9 @@
             pltpu.VMEM(observed, f32),
             pltpu.VMEM((levels * outer_rows, cols), f32),
             pltpu.VMEM((levels, 4, rows, cols), f32),
-            pltpu.VMEM((2, REACH - 2, 4, rows, cols), f32),
-            pltpu.VMEM((2, 3, rows, cols), f32),
-            pltpu.VMEM((2, 3, rows, cols), f32),
+            pltpu.VMEM((2, 4, rows, cols), f32),
+            pltpu.VMEM((2, 4 * rows // TILE + 1, TILE, cols), f32),
+            pltpu.VMEM((2, 4 * rows // TILE + 1, TILE, cols), f32),
             pltpu.VMEM((2, levels, 4, TILE, cols), f32),
             pltpu.VMEM((2, 2, 2 * TILE, cols), f32),
             pltpu.VMEM((2, 2, 2 * TILE, cols), f32),

time: 10.5 us -> 10.3 us (0.981)
  the two profiles are of different devices: /device:TPU:0 before, /device:TPU:1 now
where the time goes in v6:
time: 10.3 us; the launch traced here: 10.1 us
  Pallas kernels  9.5 us (92%)
  between operations  0.64 us (6%)
    pallas_call x1, Pallas kernels, shards(): pl.pallas_call(functools.partial(kernel, ends), out_shape=(pltpu.VMEM((le...  8.57 us
    pallas_call x1, Pallas kernels, shards(): pl.pallas_call(finish, out_shape=(jax.ShapeDtypeStruct((levels, rows, col...  0.94 us

profile of v6, /device:TPU:1, one launch (start us, length us, event | category | flops | bytes accessed | tf_op | source)
XLA Modules:
  0.0 10.1 jit_solution(3982376333365835208)
XLA Ops:
  0.6 8.6 %shard_map.76 = (f32[4,16,128]{2,1,0:T(8,128)S(1)}, f32[4,16,128]{2,1,0:T(8,128)S(1)}, bf16[256,512]{1,0:T(8,128)(2,1)S(1)}) custom-call(bf16[256,512]{1,0:T(8,128)(2,1)} %bitcast.5, bf16[3,4,16,128]{3,2,1,0:T(8,128)(2,1)} %courant_hbm.1, s32[16,128]{1,0:T(8,128)} %bitcast.6, s32[16,128]{1,0:T(8,128)} %bitcast.7, f32[16,128]{1,0:T(8,128)} %bitcast.8), custom_call_target="tpu_custom_call" | custom-call | tf_op jit(solution)/shard_map/pallas_call | solution.py:592
  9.2 0.9 %shard_map.77 = (f32[4,16,128]{2,1,0:T(8,128)}, f32[4,16,128]{2,1,0:T(8,128)}, bf16[256,512]{1,0:T(8,128)(2,1)}) custom-call(f32[4,16,128]{2,1,0:T(8,128)S(1)} %get-tuple-element.9.state_v, f32[4,16,128]{2,1,0:T(8,128)S(1)} %get-tuple-element.10.adj_v, bf16[256,512]{1,0:T(8,128)(2,1)S(1)} %get-tuple-element.11.outer), custom_call_target="tpu_custom_call" | custom-call | tf_op jit(solution)/shard_map/pallas_call | solution.py:637

commit v7 on v6

--- a/solution.py
+++ b/solution.py
@@ -62,7 +62,7 @@
     beyond = (span - levels) // 2
 
     loads = [
-        pltpu.make_async_copy(src, dst, in_sem.at[i])
+        pltpu.make_async_copy(src, dst, in_sem.at[min(i, 2)])
         for i, (src, dst) in enumerate(
             ((outer_hbm, outer), (courant_hbm, courant), (col_hbm, col), (lvl_hbm, lvl), (val_hbm, val))
         )
@@ -188,11 +188,13 @@
     lower_rest, upper_rest = [[c for c in side if len(c[0]) > 1] for side in (lower, upper)]
     lower_south = pick(lambda w: corner(w) and 1 in w and 3 in w)
     upper_north = pick(lambda w: corner(w) and 0 in w and 2 in w)
+    lower_north = pick(lambda w: corner(w) and 1 in w and 2 in w, is_behind)
+    upper_south = pick(lambda w: corner(w) and 0 in w and 3 in w, is_ahead)
     south, north = pick(lambda w: w == [3]), pick(lambda w: w == [2])
     behind, ahead = pick(level_lon, is_behind), pick(level_lon, is_ahead)
 
     barrier = pltpu.get_barrier_semaphore()
-    signal(barrier, upper_north + upper_rest + upper_face + ahead + north)
+    signal(barrier, upper_north + upper_south + upper_rest + upper_face + ahead + north)
 
     def settle(messages, flip, sem, known=()):
         if len(known) < 4:
@@ -255,16 +257,17 @@
     def at_once(w):
         return (1 in w and not (corner(w) and 2 in w)) or w == [3]
 
-    def to_north(w):
-        return w == [2] or (corner(w) and 1 in w and 2 in w)
-
-    expected = count(lower + lower_south + south + behind)
+    def north_corner(w):
+        return corner(w) and 1 in w and 2 in w
+
+    expected = count(lower + lower_south + lower_north + south + behind)
     pl.when(expected > 0)(lambda: pl.semaphore_wait(barrier, expected))
     signal(ready.at[4], [(w, is_behind(w)) for w, _ in lower_south])
     signal(ready.at[3], lower_rest)
     signal(ready.at[0], behind)
     signal(ready.at[2], lower_face)
     signal(ready.at[1], south)
+    send(first, north_corner, is_behind)
     send(first, at_once)
     send(first, level_lon, is_behind)
     send(faces, at_once)
@@ -295,8 +298,8 @@
         for n, (at, f, r) in enumerate(rim_rows(l, far)):
             deep_out[s, 4 * high, n : n + 1, :] = own[at, f, r : r + 1, :]
 
-    for load in loads[2:]:
-        load.wait()
+    view = units.at[pl.ds(0, 3 * col.shape[0])]
+    pltpu.make_async_copy(view, view, in_sem.at[2]).wait()
     where_row = (lvl[...] - me_lev * levels + beyond) * rows + col[...] // cols
     where_col = col[...] % cols
     parts = bf16_parts(val[...], 2)
@@ -330,14 +333,13 @@
     send(second, at_once)
     send(second, level_lon, is_behind)
 
-    def go_north():
+    send(faces, at_once, later=2)
+
+    @pl.when(links[2][2])
+    def _():
         pl.semaphore_wait(ready.at[1], 1)
-        send(first + faces + second, to_north)
-
-    early = me_lon > 0
-    pl.when(links[2][2] & early)(go_north)
-    send(faces, at_once, later=2)
-    pl.when(links[2][2] & jnp.logical_not(early))(go_north)
+        send(first, north_corner, is_ahead)
+        send(first + faces + second, lambda w: w == [2])
 
     @pl.when(me_lon < n_lon - 1)
     def _():
@@ -427,6 +429,7 @@
         return joined(full, seen_half[0, b, i], seen_half[1, b, i])
 
     settle(second, 1, recv_sem.at[1])
+    settle(faces, 1, recv_sem.at[2])
     side_q = []
     for side in range(2):
         known = []
@@ -449,8 +452,6 @@
     fix_v = {l: inserted(fix_v, l) for l in range(2 - near - 1, levels + near - 1)}
     fix_q = {l: inserted(fix, l) for l in range(-1, levels + 1)}
     crossing = {l: inserted(crossing, l) for l in range(levels)}
-
-    settle(faces, 1, recv_sem.at[2])
 
     speeds = {l: [cell(l, k + 1) for k in range(3)] for l in range(-1, levels + 1)}
     start = {l: cell(l, 0) for l in range(-1, levels + 1)}
@@ -621,7 +622,7 @@
             pltpu.VMEM((2, 2, rows, cols), f32),
             pltpu.VMEM((2, 3, 2, TILE, cols), f32),
             pltpu.VMEM((2048, 1, cols), f32),
-            pltpu.SemaphoreType.DMA((5,)),
+            pltpu.SemaphoreType.DMA((3,)),
             pltpu.SemaphoreType.DMA,
             pltpu.SemaphoreType.DMA((3,)),
             pltpu.SemaphoreType.REGULAR((5,)),

time: 10.3 us -> 10.1 us (0.981)
  Pallas kernels: 9.5 us -> 9.33 us
    pallas_call x1, Pallas kernels: 8.57 us -> 8.39 us  [shards(): pl.pallas_call(functools.partial(kernel, ends), out_shape=(pltpu.VMEM((le...]
where the time goes in v7:
time: 10.1 us; the launch traced here: 9.97 us
  Pallas kernels  9.33 us (92%)
  between operations  0.64 us (6%)
    pallas_call x1, Pallas kernels, shards(): pl.pallas_call(functools.partial(kernel, ends), out_shape=(pltpu.VMEM((le...  8.39 us
    pallas_call x1, Pallas kernels, shards(): pl.pallas_call(finish, out_shape=(jax.ShapeDtypeStruct((levels, rows, col...  0.94 us

profile of v7, /device:TPU:1, one launch (start us, length us, event | category | flops | bytes accessed | tf_op | source)
XLA Modules:
  0.0 10.0 jit_solution(3064646215656464339)
XLA Ops:
  0.6 8.4 %shard_map.76 = (f32[4,16,128]{2,1,0:T(8,128)S(1)}, f32[4,16,128]{2,1,0:T(8,128)S(1)}, bf16[256,512]{1,0:T(8,128)(2,1)S(1)}) custom-call(bf16[256,512]{1,0:T(8,128)(2,1)} %bitcast.5, bf16[3,4,16,128]{3,2,1,0:T(8,128)(2,1)} %courant_hbm.1, s32[16,128]{1,0:T(8,128)} %bitcast.6, s32[16,128]{1,0:T(8,128)} %bitcast.7, f32[16,128]{1,0:T(8,128)} %bitcast.8), custom_call_target="tpu_custom_call" | custom-call | tf_op jit(solution)/shard_map/pallas_call | solution.py:593
  9.0 0.9 %shard_map.77 = (f32[4,16,128]{2,1,0:T(8,128)}, f32[4,16,128]{2,1,0:T(8,128)}, bf16[256,512]{1,0:T(8,128)(2,1)}) custom-call(f32[4,16,128]{2,1,0:T(8,128)S(1)} %get-tuple-element.9.state_v, f32[4,16,128]{2,1,0:T(8,128)S(1)} %get-tuple-element.10.adj_v, bf16[256,512]{1,0:T(8,128)(2,1)S(1)} %get-tuple-element.11.outer), custom_call_target="tpu_custom_call" | custom-call | tf_op jit(solution)/shard_map/pallas_call | solution.py:638

commit v8 on v7

--- a/solution.py
+++ b/solution.py
@@ -30,12 +30,19 @@
     return result
 
 
+def again(v, c, minus, plus):
+    result = centre_of(c) * v
+    for k in range(3):
+        low = jnp.maximum(c[k], 0.0)
+        result = result + low * minus[k] + (low - c[k]) * plus[k]
+    return result
+
+
 def shares(p, c):
     low, up = [], []
     for n in c:
-        moved = jnp.abs(n) * p
-        low.append(jnp.where(n > 0.0, moved, 0.0))
-        up.append(jnp.where(n > 0.0, 0.0, moved))
+        low.append(jnp.maximum(n, 0.0) * p)
+        up.append(low[-1] - n * p)
     return low, up
 
 
@@ -142,12 +149,12 @@
                     first.append(Message(which, strip.at[pl.ds(*bands[t])], strip_half.at[a, t, b], 0))
                 if u is None:
                     if a and t is None:
-                        faces.append(Message(which, own.at[levels - 1 if a == 1 else 0], face_in.at[a - 1], 2))
-                        faces.append(Message(which, deep_out.at[a - 1], deep_in.at[a - 1], 2, 2))
+                        faces.append(Message(which, own.at[levels - 1 if a == 1 else 0], face_in.at[a - 1], 1))
+                        faces.append(Message(which, deep_out.at[a - 1], deep_in.at[a - 1], 1, 2))
                     elif a:
                         first.append(Message(which, edge_out.at[a - 1, t], edge_in.at[a - 1, t], 0))
                     else:
-                        faces.append(Message(which, own.at[:, :, pl.ds(*bands[t])], side_in.at[t], 2))
+                        first.append(Message(which, own.at[:, :, pl.ds(*bands[t])], side_in.at[t], 0))
                 if not a:
                     if t is None:
                         second.append(Message(which, seen_strip, seen_full.at[u], 1))
@@ -156,7 +163,7 @@
                     if u is None:
                         kept = pl.ds(1, span - 2)
                         second.append(Message(which, seen.at[kept, :, pl.ds(*bands[t])], seen_in.at[t], 1))
-    first.sort(key=lambda m: -len(m.target))
+    first.sort(key=lambda m: m.lines() - 1024 * len(m.target))
 
     def pick(test, side=None):
         return [(which, None if side is None else side(which)) for which in partners if test(which)]
@@ -194,7 +201,7 @@
     behind, ahead = pick(level_lon, is_behind), pick(level_lon, is_ahead)
 
     barrier = pltpu.get_barrier_semaphore()
-    signal(barrier, upper_north + upper_south + upper_rest + upper_face + ahead + north)
+    signal(barrier, upper_rest[::-1] + upper_north + upper_face + ahead + upper_south + north)
 
     def settle(messages, flip, sem, known=()):
         if len(known) < 4:
@@ -339,7 +346,7 @@
     def _():
         pl.semaphore_wait(ready.at[1], 1)
         send(first, north_corner, is_ahead)
-        send(first + faces + second, lambda w: w == [2])
+        send(first + second, lambda w: w == [2])
 
     @pl.when(me_lon < n_lon - 1)
     def _():
@@ -428,8 +435,23 @@
         full = seen_strip[i] if b == 0 else seen_full[b - 1, i]
         return joined(full, seen_half[0, b, i], seen_half[1, b, i])
 
-    settle(second, 1, recv_sem.at[1])
-    settle(faces, 1, recv_sem.at[2])
+    speeds = {l: [cell(l, k + 1) for k in range(3)] for l in range(levels)}
+    start = {l: cell(l, 0) for l in range(levels)}
+
+    def lev_term(v, l):
+        n = speeds[l][0]
+        return jnp.abs(n) * jnp.where(n > 0.0, v[l - 1], v[l + 1])
+
+    def within(v, l):
+        result = centre_of(speeds[l]) * v[l]
+        for n, minus, plus in zip(speeds[l][1:], (down(v[l]), right(v[l])), (up_row(v[l]), left(v[l]))):
+            result = result + jnp.abs(n) * jnp.where(n > 0.0, minus, plus)
+        return result
+
+    begun = {l: within(start, l) for l in range(levels)}
+    begun = {l: begun[l] + lev_term(start, l) if 0 < l < levels - 1 else begun[l] for l in begun}
+
+    settle(second + faces, 1, recv_sem.at[1])
     side_q = []
     for side in range(2):
         known = []
@@ -453,8 +475,9 @@
     fix_q = {l: inserted(fix, l) for l in range(-1, levels + 1)}
     crossing = {l: inserted(crossing, l) for l in range(levels)}
 
-    speeds = {l: [cell(l, k + 1) for k in range(3)] for l in range(-1, levels + 1)}
-    start = {l: cell(l, 0) for l in range(-1, levels + 1)}
+    for l in (-1, levels):
+        speeds[l] = [cell(l, k + 1) for k in range(3)]
+        start[l] = cell(l, 0)
     beside = ((-2, -1, -3), (levels + 1, levels, levels + 2))
 
     def deep(s, n):
@@ -471,8 +494,8 @@
         below = jnp.where((row == rows - 1) & (c <= 0.0), up_row(x)[:rows], 0.0)
         return jnp.abs(c) * (above + below)
 
-    def step(v, l):
-        return forward(v[l], speeds[l], [v[l - 1], down(v[l]), right(v[l])], [v[l + 1], up_row(v[l]), left(v[l])])
+    def step(v, l, rule=forward):
+        return rule(v[l], speeds[l], [v[l - 1], down(v[l]), right(v[l])], [v[l + 1], up_row(v[l]), left(v[l])])
 
     outside = []
     for s, (l, _, far) in enumerate(beside):
@@ -487,10 +510,12 @@
         gained = across(c[1], start[l])
         further = across(kept_rows(s, ((6, 0), (7, rows - 1))), start[far])
         outside.append((c, gained, further))
-    v = {l: step(start, l) for l in range(-1, levels + 1)}
+    v = {l: step(start, l) for l in (-1, levels)}
+    for l in range(levels):
+        v[l] = begun[l] if 0 < l < levels - 1 else begun[l] + lev_term(start, l)
     for s, (l, _, _) in enumerate(beside):
         v[l] = jnp.concatenate([deep(s, 1) + outside[s][1], step(start, l)[rows:]], axis=0)
-    second_v = {l: step(v, l) for l in range(-1, levels + 1)}
+    second_v = {l: step(v, l, again) for l in range(-1, levels + 1)}
     for s, (l, by, _) in enumerate(beside):
         c, gained, further = outside[s]
         sizes = [jnp.abs(n) for n in c]
@@ -624,7 +649,7 @@
             pltpu.VMEM((2048, 1, cols), f32),
             pltpu.SemaphoreType.DMA((3,)),
             pltpu.SemaphoreType.DMA,
-            pltpu.SemaphoreType.DMA((3,)),
+            pltpu.SemaphoreType.DMA((2,)),
             pltpu.SemaphoreType.REGULAR((5,)),
         ],
         compiler_params=pltpu.CompilerParams(collective_id=0, has_side_effects=True),

time: 10.1 us -> 10.1 us (level)
  the two profiles are of different devices: /device:TPU:1 before, /device:TPU:0 now
where the time goes in v8:
time: 10.1 us; the launch traced here: 9.87 us
  Pallas kernels  9.23 us (91%)
  between operations  0.64 us (6%)
    pallas_call x1, Pallas kernels, shards(): pl.pallas_call(functools.partial(kernel, ends), out_shape=(pltpu.VMEM((le...  8.29 us
    pallas_call x1, Pallas kernels, shards(): pl.pallas_call(finish, out_shape=(jax.ShapeDtypeStruct((levels, rows, col...  0.94 us

profile of v8, /device:TPU:0, one launch (start us, length us, event | category | flops | bytes accessed | tf_op | source)
XLA Modules:
  0.0 9.9 jit_solution(12508145049760197178)
XLA Ops:
  0.6 8.3 %shard_map.76 = (f32[4,16,128]{2,1,0:T(8,128)S(1)}, f32[4,16,128]{2,1,0:T(8,128)S(1)}, bf16[256,512]{1,0:T(8,128)(2,1)S(1)}) custom-call(bf16[256,512]{1,0:T(8,128)(2,1)} %bitcast.5, bf16[3,4,16,128]{3,2,1,0:T(8,128)(2,1)} %courant_hbm.1, s32[16,128]{1,0:T(8,128)} %bitcast.6, s32[16,128]{1,0:T(8,128)} %bitcast.7, f32[16,128]{1,0:T(8,128)} %bitcast.8), custom_call_target="tpu_custom_call" | custom-call | tf_op jit(solution)/shard_map/pallas_call | solution.py:618
  8.9 0.9 %shard_map.77 = (f32[4,16,128]{2,1,0:T(8,128)}, f32[4,16,128]{2,1,0:T(8,128)}, bf16[256,512]{1,0:T(8,128)(2,1)}) custom-call(f32[4,16,128]{2,1,0:T(8,128)S(1)} %get-tuple-element.9.state_v, f32[4,16,128]{2,1,0:T(8,128)S(1)} %get-tuple-element.10.adj_v, bf16[256,512]{1,0:T(8,128)(2,1)S(1)} %get-tuple-element.11.outer), custom_call_target="tpu_custom_call" | custom-call | tf_op jit(solution)/shard_map/pallas_call | solution.py:663

commit v9 on v8

--- a/solution.py
+++ b/solution.py
@@ -291,19 +291,6 @@
     def rim_rows(second_level, third_level):
         kept = [(second_level, 2, r) for r in (0, 1, rows - 2, rows - 1)]
         return kept + [(second_level, 3, r) for r in (0, rows - 1)] + [(third_level, 2, r) for r in (0, rows - 1)]
-
-    pairs = ((levels - 2, levels - 3), (1, 2))
-    once = {
-        l: inner(own[l, 0], [own[l, k + 1] for k in range(3)], own[l - 1, 0], own[l + 1, 0])
-        for l in sorted(set(pairs[0] + pairs[1]))
-    }
-    for s, (l, far) in enumerate(pairs):
-        c = [own[l, k + 1] for k in range(3)]
-        twice = inner(once[l], c, zero if s else once[far], once[far] if s else zero)
-        for n, plane in enumerate((own[l, 0], once[l], twice, c[0])):
-            deep_out[s, n * high : (n + 1) * high] = plane.reshape(high, TILE, cols)
-        for n, (at, f, r) in enumerate(rim_rows(l, far)):
-            deep_out[s, 4 * high, n : n + 1, :] = own[at, f, r : r + 1, :]
 
     view = units.at[pl.ds(0, 3 * col.shape[0])]
     pltpu.make_async_copy(view, view, in_sem.at[2]).wait()
@@ -340,6 +327,19 @@
     send(second, at_once)
     send(second, level_lon, is_behind)
 
+    pairs = ((levels - 2, levels - 3), (1, 2))
+    once = {
+        l: inner(own[l, 0], [own[l, k + 1] for k in range(3)], own[l - 1, 0], own[l + 1, 0])
+        for l in sorted(set(pairs[0] + pairs[1]))
+    }
+    for s, (l, far) in enumerate(pairs):
+        c = [own[l, k + 1] for k in range(3)]
+        twice = inner(once[l], c, zero if s else once[far], once[far] if s else zero)
+        for n, plane in enumerate((own[l, 0], once[l], twice, c[0])):
+            deep_out[s, n * high : (n + 1) * high] = plane.reshape(high, TILE, cols)
+        for n, (at, f, r) in enumerate(rim_rows(l, far)):
+            deep_out[s, 4 * high, n : n + 1, :] = own[at, f, r : r + 1, :]
+
     send(faces, at_once, later=2)
 
     @pl.when(links[2][2])
@@ -451,6 +451,7 @@
     begun = {l: within(start, l) for l in range(levels)}
     begun = {l: begun[l] + lev_term(start, l) if 0 < l < levels - 1 else begun[l] for l in begun}
 
+    settle(first + second + faces, 0, send_sem)
     settle(second + faces, 1, recv_sem.at[1])
     side_q = []
     for side in range(2):
@@ -559,8 +560,6 @@
         total = total + jnp.where(rim, crossing[l], 0.0)
         total = total + jnp.where(lanes >= cols - 1, 0.0, left(low[l][2])) + jnp.where(lanes < 1, 0.0, right(up[l][2]))
         adj_v[l] = total[:rows]
-
-    settle(first + second + faces, 0, send_sem)
 
 
 def finish(state_v, adj_v, outer, state_hbm, adj_hbm, next_hbm, wide, nxt, out_sem):

time: 10.1 us -> 10 us (0.990); the launches traced: 9.87 us -> 9.89 us
  no operation moved by 1% of the time
where the time goes in v9:
time: 10 us; the launch traced here: 9.89 us
  Pallas kernels  9.25 us (92%)
  between operations  0.64 us (6%)
    pallas_call x1, Pallas kernels, shards(): pl.pallas_call(functools.partial(kernel, ends), out_shape=(pltpu.VMEM((le...  8.31 us
    pallas_call x1, Pallas kernels, shards(): pl.pallas_call(finish, out_shape=(jax.ShapeDtypeStruct((levels, rows, col...  0.94 us

profile of v9, /device:TPU:0, one launch (start us, length us, event | category | flops | bytes accessed | tf_op | source)
XLA Modules:
  0.0 9.9 jit_solution(13325517934315799761)
XLA Ops:
  0.6 8.3 %shard_map.76 = (f32[4,16,128]{2,1,0:T(8,128)S(1)}, f32[4,16,128]{2,1,0:T(8,128)S(1)}, bf16[256,512]{1,0:T(8,128)(2,1)S(1)}) custom-call(bf16[256,512]{1,0:T(8,128)(2,1)} %bitcast.5, bf16[3,4,16,128]{3,2,1,0:T(8,128)(2,1)} %courant_hbm.1, s32[16,128]{1,0:T(8,128)} %bitcast.6, s32[16,128]{1,0:T(8,128)} %bitcast.7, f32[16,128]{1,0:T(8,128)} %bitcast.8), custom_call_target="tpu_custom_call" | custom-call | tf_op jit(solution)/shard_map/pallas_call | solution.py:617
  9.0 0.9 %shard_map.77 = (f32[4,16,128]{2,1,0:T(8,128)}, f32[4,16,128]{2,1,0:T(8,128)}, bf16[256,512]{1,0:T(8,128)(2,1)}) custom-call(f32[4,16,128]{2,1,0:T(8,128)S(1)} %get-tuple-element.9.state_v, f32[4,16,128]{2,1,0:T(8,128)S(1)} %get-tuple-element.10.adj_v, bf16[256,512]{1,0:T(8,128)(2,1)S(1)} %get-tuple-element.11.outer), custom_call_target="tpu_custom_call" | custom-call | tf_op jit(solution)/shard_map/pallas_call | solution.py:662

commit v10 on v9

--- a/solution.py
+++ b/solution.py
@@ -324,8 +324,8 @@
             place = g + REACH - beyond
             ends_only = jnp.where(group == place, pltpu.roll(values[g], (REACH + GROUP * place) % cols, axis=1), ends_only)
         seen_strip[i] = ends_only
+    send(second, level_lon, is_behind)
     send(second, at_once)
-    send(second, level_lon, is_behind)
 
     pairs = ((levels - 2, levels - 3), (1, 2))
     once = {

time: 10 us -> 10 us (level)
  no operation moved by 1% of the time
where the time goes in v10:
time: 10 us; the launch traced here: 9.89 us
  Pallas kernels  9.25 us (92%)
  between operations  0.64 us (6%)
    pallas_call x1, Pallas kernels, shards(): pl.pallas_call(functools.partial(kernel, ends), out_shape=(pltpu.VMEM((le...  8.31 us
    pallas_call x1, Pallas kernels, shards(): pl.pallas_call(finish, out_shape=(jax.ShapeDtypeStruct((levels, rows, col...  0.94 us

profile of v10, /device:TPU:0, one launch (start us, length us, event | category | flops | bytes accessed | tf_op | source)
XLA Modules:
  0.0 9.9 jit_solution(1788260539206881241)
XLA Ops:
  0.6 8.3 %shard_map.76 = (f32[4,16,128]{2,1,0:T(8,128)S(1)}, f32[4,16,128]{2,1,0:T(8,128)S(1)}, bf16[256,512]{1,0:T(8,128)(2,1)S(1)}) custom-call(bf16[256,512]{1,0:T(8,128)(2,1)} %bitcast.5, bf16[3,4,16,128]{3,2,1,0:T(8,128)(2,1)} %courant_hbm.1, s32[16,128]{1,0:T(8,128)} %bitcast.6, s32[16,128]{1,0:T(8,128)} %bitcast.7, f32[16,128]{1,0:T(8,128)} %bitcast.8), custom_call_target="tpu_custom_call" | custom-call | tf_op jit(solution)/shard_map/pallas_call | solution.py:617
  9.0 0.9 %shard_map.77 = (f32[4,16,128]{2,1,0:T(8,128)}, f32[4,16,128]{2,1,0:T(8,128)}, bf16[256,512]{1,0:T(8,128)(2,1)}) custom-call(f32[4,16,128]{2,1,0:T(8,128)S(1)} %get-tuple-element.9.state_v, f32[4,16,128]{2,1,0:T(8,128)S(1)} %get-tuple-element.10.adj_v, bf16[256,512]{1,0:T(8,128)(2,1)S(1)} %get-tuple-element.11.outer), custom_call_target="tpu_custom_call" | custom-call | tf_op jit(solution)/shard_map/pallas_call | solution.py:662

commit v11 on v10

--- a/solution.py
+++ b/solution.py
@@ -275,8 +275,8 @@
     signal(ready.at[2], lower_face)
     signal(ready.at[1], south)
     send(first, north_corner, is_behind)
+    send(first, level_lon, is_behind)
     send(first, at_once)
-    send(first, level_lon, is_behind)
     send(faces, at_once)
 
     row = lax.broadcasted_iota(jnp.int32, (rows, cols), 0)

time: 10 us -> 10 us (level)
  no operation moved by 1% of the time
where the time goes in v11:
time: 10 us; the launch traced here: 9.89 us
  Pallas kernels  9.25 us (92%)
  between operations  0.64 us (6%)
    pallas_call x1, Pallas kernels, shards(): pl.pallas_call(functools.partial(kernel, ends), out_shape=(pltpu.VMEM((le...  8.31 us
    pallas_call x1, Pallas kernels, shards(): pl.pallas_call(finish, out_shape=(jax.ShapeDtypeStruct((levels, rows, col...  0.94 us

profile of v11, /device:TPU:0, one launch (start us, length us, event | category | flops | bytes accessed | tf_op | source)
XLA Modules:
  0.0 9.9 jit_solution(2541098095676555239)
XLA Ops:
  0.6 8.3 %shard_map.76 = (f32[4,16,128]{2,1,0:T(8,128)S(1)}, f32[4,16,128]{2,1,0:T(8,128)S(1)}, bf16[256,512]{1,0:T(8,128)(2,1)S(1)}) custom-call(bf16[256,512]{1,0:T(8,128)(2,1)} %bitcast.5, bf16[3,4,16,128]{3,2,1,0:T(8,128)(2,1)} %courant_hbm.1, s32[16,128]{1,0:T(8,128)} %bitcast.6, s32[16,128]{1,0:T(8,128)} %bitcast.7, f32[16,128]{1,0:T(8,128)} %bitcast.8), custom_call_target="tpu_custom_call" | custom-call | tf_op jit(solution)/shard_map/pallas_call | solution.py:617
  9.0 0.9 %shard_map.77 = (f32[4,16,128]{2,1,0:T(8,128)}, f32[4,16,128]{2,1,0:T(8,128)}, bf16[256,512]{1,0:T(8,128)(2,1)}) custom-call(f32[4,16,128]{2,1,0:T(8,128)S(1)} %get-tuple-element.9.state_v, f32[4,16,128]{2,1,0:T(8,128)S(1)} %get-tuple-element.10.adj_v, bf16[256,512]{1,0:T(8,128)(2,1)S(1)} %get-tuple-element.11.outer), custom_call_target="tpu_custom_call" | custom-call | tf_op jit(solution)/shard_map/pallas_call | solution.py:662
